TPU v7x, 128 devices: a whole 4x4x4 slice. The times are simulated.
128 devices in a mesh: shard: 16 (over x_hi, z, core), rep: 8 (over x_lo, y).
Axes of the slice: x: 4 (x_hi: 2, x_lo: 2; x = x_hi * 2 + x_lo), y: 4, z: 4, core: 2. Of those that a mesh axis runs over, the one named last changes fastest.
Arguments:
- tokens: bfloat16 [49152, 5120], P(('shard', 'rep')), may hold values from -700 to 700
- norm_gain: float32 [5120], replicated, may hold values from 0.1 to 1.9
- key_bias: float32 [1024], replicated, may hold values from -4 to 4
- key_weight: bfloat16 [8192, 1024], P('shard'), may hold values from -0.078125 to 0.078125
- cotangent: bfloat16 [49152, 1024], P(('shard', 'rep')), may hold values from -40 to 40
- block_slot: int32 [40], replicated, may hold values from 0 to 63, as said below
Outputs:
- projected: bfloat16 [49152, 1024], P(('shard', 'rep'))
- token_grad: bfloat16 [49152, 5120], P(('shard', 'rep'))
- weight_grad: float32 [8192, 1024], P('shard')
- gain_grad: float32 [5120], replicated
- bias_grad: float32 [1024], replicated
Inputs may be any that keep to these rules, and one draw needn't show every extreme that they name: Entries are distinct; block b lies on the device of shard with index block_slot[b] // 4, at its local slot block_slot[b] % 4; in every draw some device holds 4 blocks.
All inputs are finite; a program needn't handle non-finite values.
Results may differ from a plain program's by a relative error of at most 0.013.
Values may be sent and summed in bfloat16 or wider, within the bound.
No kernel may reach another device: no remote copies, remote signals or barrier semaphores. Data moves between devices by JAX's collectives and lax.ppermute only.
A program may use at most 128 MiB of HBM per device.

v0:
```python
import jax
import jax.numpy as jnp
from jax import lax
from jax.experimental import pallas as pl
from jax.experimental.pallas import tpu as pltpu
from jax.sharding import PartitionSpec as P

BLK = 128
EPS = 1e-06
AXES = ("shard", "rep")
BF = jnp.bfloat16
F32 = jnp.float32


def _flat(x, y, z, c):
    return ((x // 2) * 8 + z * 2 + c) * 8 + (x % 2) * 4 + y


def _pairs(move):
    return [
        (_flat(x, y, z, c), _flat(*move(x, y, z, c)))
        for x in range(4)
        for y in range(4)
        for z in range(4)
        for c in range(2)
    ]


def _turn(axis, k, place):
    place = list(place)
    place[axis] = (place[axis] + k) % 4
    return tuple(place)


def _send(v, move):
    return lax.ppermute(v, AXES, _pairs(move))


def send_core(v):
    return _send(v, lambda x, y, z, c: (x, y, z, 1 - c))


X, Y, Z = 0, 1, 2
STAGE = {"a": (Y, Z), "b": (Z, Y)}
SHIFTS = (1, 3, 2)


def send_on(axes, v, k):
    return _send(v, lambda *p: _turn(axes[p[3]], k, p[:3]) + (p[3],))


def inv_rms_of(values):
    return lax.rsqrt(jnp.mean(values * values, axis=-1, keepdims=True) + EPS)


CHUNK = 1280
STRIP = 1280


def _cols(tile):
    return pl.ds(pl.multiple_of(tile * BLK, BLK), BLK)


def _terms_kernel(scale, tiles, inv, other_inv, cot, other_cot, own, other, gain, *rest):
    outs, pair = rest[:7], rest[7]
    rows, width = own.shape
    steps = width // STRIP
    for i in range(4):
        pair[:rows, i * BLK : (i + 1) * BLK] = cot[:, _cols(tiles[i])]
        pair[rows:, i * BLK : (i + 1) * BLK] = other_cot[:, _cols(tiles[i])]

    def body(at, own, other, gain, *parts):
        j = at.index[0]
        g = gain[...]
        one = (own[...].astype(F32) * inv[...] * g).astype(BF)
        two = (other[...].astype(F32) * other_inv[...] * g).astype(BF)
        terms = lax.dot_general(
            jnp.concatenate([one, two]),
            pair[...],
            (((0,), (0,)), ((), ())),
            preferred_element_type=F32,
        )
        terms = (terms * scale).astype(BF)
        parts[0][...] = terms[:, :BLK]

        @pl.when(j < steps // 2)
        def _():
            for i in range(1, 4):
                parts[2 * i - 1][...] = terms[:, i * BLK : (i + 1) * BLK]

        @pl.when(j >= steps // 2)
        def _():
            for i in range(1, 4):
                parts[2 * i][...] = terms[:, i * BLK : (i + 1) * BLK]

    strip = lambda j: (0, j)
    top = steps // 2
    upper = pl.BlockSpec((STRIP, BLK), lambda j: (jnp.minimum(j, top - 1), 0))
    lower = pl.BlockSpec((STRIP, BLK), lambda j: (jnp.maximum(j - top, 0), 0))
    pltpu.emit_pipeline(
        body,
        grid=(width // STRIP,),
        in_specs=[
            pl.BlockSpec((rows, STRIP), strip),
            pl.BlockSpec((rows, STRIP), strip),
            pl.BlockSpec((1, STRIP), strip),
        ],
        out_specs=[pl.BlockSpec((STRIP, BLK), lambda j: (j, 0))] + [upper, lower] * 3,
        _explicit_indices=True,
    )(own, other, gain, *outs)


def weight_terms(scale, tiles, own, other, inv, other_inv, gain, cot, other_cot):
    rows, width = own.shape
    vmem = pl.BlockSpec(memory_space=pltpu.VMEM)
    hbm = pl.BlockSpec(memory_space=pltpu.HBM)
    return pl.pallas_call(
        lambda *refs: _terms_kernel(scale, *refs),
        in_specs=[pl.BlockSpec(memory_space=pltpu.SMEM)] + [vmem] * 4 + [hbm] * 3,
        out_specs=[hbm] * 7,
        scratch_shapes=[pltpu.VMEM((2 * rows, 4 * BLK), BF)],
        out_shape=[jax.ShapeDtypeStruct((width, BLK), BF)]
        + [jax.ShapeDtypeStruct((width // 2, BLK), BF)] * 6,
        compiler_params=pltpu.CompilerParams(vmem_limit_bytes=56 * 1024 * 1024),
        name="weight_terms",
    )(tiles, inv, other_inv, cot, other_cot, own, other, gain)


def _tokens_kernel(tiles, tok, inv, gain, bias, cot, *rest):
    pieces, (proj, grad) = rest[:10], rest[10:12]
    turned, weight, acc, scaled, out, sems = rest[12:]
    _, width = tok.shape
    chunks = width // CHUNK
    for i in range(8):
        turned[:, i * BLK : (i + 1) * BLK] = cot[:, _cols(tiles[i])]
    r = inv[...]
    for j in range(chunks):
        at = slice(j * CHUNK, (j + 1) * CHUNK)
        for i in range(8):
            first = 5 * (i // 4) + i % 4
            piece, rows_at = pieces[first], at
            if i % 4 == 3 and j >= chunks // 2:
                half = chunks // 2 * CHUNK
                piece, rows_at = pieces[first + 1], slice(at.start - half, at.stop - half)
            weight[:, i * BLK : (i + 1) * BLK] = piece[rows_at]
        g = gain[:, at]
        normed = (tok[:, at].astype(F32) * r * g).astype(BF)
        part = jnp.dot(normed, weight[...], preferred_element_type=F32)
        if j == 0:
            acc[...] = part
        else:
            acc[...] += part
        grad_normed = lax.dot_general(
            turned[...], weight[...], (((1,), (1,)), ((), ())), preferred_element_type=F32
        )
        scaled[j] = grad_normed * g
    for i in range(8):
        cols = _cols(tiles[i])
        proj[:, cols] = (acc[:, i * BLK : (i + 1) * BLK] + bias[:, cols]).astype(BF)
    along = jnp.sum(acc[...] * turned[...].astype(F32), axis=1, keepdims=True)
    back = r * along * (1.0 / width)
    copies = []
    for j in range(chunks):
        at = slice(j * CHUNK, (j + 1) * CHUNK)
        out[j] = (r * (scaled[j] - tok[:, at].astype(F32) * back)).astype(BF)
        copies.append(pltpu.make_async_copy(out.at[j], grad.at[:, at], sems.at[j]))
        copies[-1].start()
    for copy in copies:
        copy.wait()


def token_work(tiles, tokens, inv, gain, bias, cot, pieces):
    rows, width = tokens.shape
    kvw = cot.shape[1]
    chunks = width // CHUNK
    vmem = pl.BlockSpec(memory_space=pltpu.VMEM)
    return pl.pallas_call(
        _tokens_kernel,
        in_specs=[pl.BlockSpec(memory_space=pltpu.SMEM)] + [vmem] * (5 + len(pieces)),
        out_specs=[vmem, pl.BlockSpec(memory_space=pltpu.HBM)],
        scratch_shapes=[
            pltpu.VMEM((rows, kvw), BF),
            pltpu.VMEM((CHUNK, kvw), BF),
            pltpu.VMEM((rows, kvw), F32),
            pltpu.VMEM((chunks, rows, CHUNK), F32),
            pltpu.VMEM((chunks, rows, CHUNK), BF),
            pltpu.SemaphoreType.DMA((chunks,)),
        ],
        out_shape=[
            jax.ShapeDtypeStruct((rows, kvw), BF),
            jax.ShapeDtypeStruct((rows, width), BF),
        ],
        compiler_params=pltpu.CompilerParams(vmem_limit_bytes=40 * 1024 * 1024),
        name="token_work",
    )(tiles, tokens, inv, gain, bias, cot, *pieces)


def small_kernel(body, outs, scalars, arrays, scratch=()):
    smem = pl.BlockSpec(memory_space=pltpu.SMEM)
    vmem = pl.BlockSpec(memory_space=pltpu.VMEM)
    return pl.pallas_call(
        body,
        in_specs=[smem] * len(scalars) + [vmem] * len(arrays),
        out_specs=[vmem] * len(outs),
        out_shape=[jax.ShapeDtypeStruct(*o) for o in outs],
        scratch_shapes=list(scratch),
    )(*scalars, *arrays)


def hi_lo(v):
    hi = v.astype(BF)
    return hi, (v - hi.astype(F32)).astype(BF)


def _place_kernel(index, one, two, three, four, out):
    for i, piece in enumerate((one, two, three, four)):
        out[:, index[i]] = piece[...]


def _merge_kernel(one, two, three, four, left, right):
    left[...] = (one[...].astype(F32) + two[...].astype(F32)).astype(BF)
    right[...] = (three[...].astype(F32) + four[...].astype(F32)).astype(BF)


def _split_kernel(index, own, top_1, top_2, bottom_1, bottom_2, *outs):
    half = top_1.shape[0]
    for i in range(4):
        at = index[i]
        total = own[:half, at].astype(F32) + top_1[:, at].astype(F32) + top_2[:, at].astype(F32)
        outs[i][:half] = total.astype(BF)
        total = own[half:, at].astype(F32) + bottom_1[:, at].astype(F32)
        outs[i][half:] = (total + bottom_2[:, at].astype(F32)).astype(BF)


def _owners_kernel(block_of_slot, row_block, one, two, three, four, w_rows, bias, out, blocks):
    nblk, rows, _ = one.shape
    total = one[...].astype(F32) + two[...].astype(F32)
    total += three[...].astype(F32) + four[...].astype(F32)
    blocks[:nblk] = total.astype(BF)
    blocks[nblk] = jnp.zeros((rows, BLK), BF)
    terms = jnp.sum(total * w_rows[...].astype(F32), axis=-1, keepdims=True)
    shape = (nblk, rows, BLK)
    lane = lax.broadcasted_iota(jnp.int32, shape, 2)
    row = lax.broadcasted_iota(jnp.int32, shape, 1)
    terms = jnp.where(lane == row + row_block[0] * rows, jnp.broadcast_to(terms, shape), 0.0)
    gain = jnp.sum(terms, axis=1).astype(BF)
    dests = out.shape[0]
    cap = block_of_slot.shape[0] // dests
    for dest in range(dests):
        for i in range(cap):
            out[dest, i * rows : (i + 1) * rows] = blocks[block_of_slot[dest * cap + i]]
        out[dest, cap * rows : cap * rows + nblk] = gain
        out[dest, cap * rows + nblk :] = bias[...]


def _pack(out, n, sums):
    hi, lo = hi_lo(sums)
    m = sums.shape[0]
    out[n : n + m] = hi
    out[n + m :] = lo


def _unpack(ref, n):
    m = (ref.shape[0] - n) // 2
    return ref[n : n + m].astype(F32) + ref[n + m :].astype(F32)


def _group_kernel(nblk, got, out):
    half = got.shape[0] // 2
    own = got.shape[1] - nblk - 16
    for i in range(half):
        pair = got[i, :own].astype(F32) + got[half + i, :own].astype(F32)
        out[i * own : (i + 1) * own] = pair.astype(BF)
    extra = jnp.sum(got[:, own:].astype(F32), axis=0)
    sums = jnp.concatenate([extra[:nblk], extra[nblk : nblk + 8] + extra[nblk + 8 :]])
    _pack(out, half * own, sums)


def _pair_kernel(n, one, two, out):
    out[:n] = (one[:n].astype(F32) + two[:n].astype(F32)).astype(BF)
    _pack(out, n, _unpack(one, n) + _unpack(two, n))


def _finish_kernel(n, cap, index, one, two, three, four, norm_gain, grad, gain, bias):
    sums = jnp.zeros((one.shape[0] - n, BLK), F32)[: (one.shape[0] - n) // 2]
    for i, piece in enumerate((one, two, three, four)):
        at = index[i]
        for z in range(4):
            for slot in range(cap):
                row = z * 2 * cap * 32 + slot * 32
                grad[slot * BLK + z * 32 : slot * BLK + z * 32 + 32, _cols(at)] = piece[
                    row : row + 32
                ].astype(F32)
                row += cap * 32
                rows = pl.ds(pl.multiple_of(slot * BLK + at * 32, 32), 32)
                grad[rows, (4 + z) * BLK : (5 + z) * BLK] = piece[row : row + 32].astype(F32)
        sums += _unpack(piece, n)
    nblk = norm_gain.shape[0]
    gain[...] = sums[:nblk] / norm_gain[...]
    bias[...] = sums[nblk:]


def local(tokens, norm_gain, key_bias, key_weight, cotangent, block_slot):
    rows, width = tokens.shape
    kvw = cotangent.shape[1]
    shards = lax.axis_size("shard")
    replicas = lax.axis_size("rep")
    cap = key_weight.shape[0] // BLK
    slots = shards * cap
    nblk = width // BLK
    grad_scale = float(rows * shards * replicas) ** (-0.5)
    s = lax.axis_index("shard")
    r = lax.axis_index("rep")
    core, z, xh = s & 1, (s >> 1) & 3, s >> 3
    xl, y = r >> 2, r & 3
    x = xh * 2 + xl
    place = (x, y, z)

    def along(axes, c=core):
        return jnp.where(c == 0, place[axes[0]], place[axes[1]])

    lag = jnp.array([0, 1, 3, 2], jnp.int32)
    me_a, me_b = (along(STAGE[stage]) for stage in "ab")
    order = jnp.concatenate(
        [4 * core + ((me_a - lag) & 3), 4 * (1 - core) + ((along(STAGE["a"], 1 - core) - lag) & 3)]
    )
    block_of_slot = (
        jnp.full((slots,), nblk, jnp.int32)
        .at[block_slot]
        .set(jnp.arange(nblk, dtype=jnp.int32))
    )

    other_tokens = send_core(tokens)
    other_cot = send_core(cotangent)
    inv_rms = inv_rms_of(tokens.astype(F32))
    other_inv = send_core(inv_rms)
    gain_row = norm_gain.reshape(1, width)
    terms = weight_terms(
        grad_scale,
        4 * core + ((me_a + lag) & 3),
        tokens,
        other_tokens,
        inv_rms,
        other_inv,
        gain_row,
        cotangent,
        other_cot,
    )
    bias_part = jnp.sum(cotangent.astype(F32), axis=0) * grad_scale
    bias_hi = lax.reduce_precision(bias_part, 8, 7)
    bias_rows = jnp.concatenate([bias_hi, bias_part - bias_hi]).astype(BF).reshape(16, BLK)
    four_parts = (nblk, 4, 32, BLK)
    own, top_1, bottom_1, top_3, bottom_3, top_2, bottom_2 = terms
    via_1 = send_on(STAGE["a"], top_2, 1)
    via_3 = send_on(STAGE["a"], bottom_2, 3)
    bottom_in = send_on(STAGE["a"], bottom_1, 1)
    top_in = send_on(STAGE["a"], top_3, 3)
    half_part = ((width // 2, BLK), BF)
    top_1, bottom_3 = small_kernel(
        _merge_kernel, [half_part] * 2, [], [top_1, via_1, bottom_3, via_3]
    )
    terms = [
        own, top_in, send_on(STAGE["a"], top_1, 1), bottom_in, send_on(STAGE["a"], bottom_3, 3)
    ]

    w_tiles = key_weight.reshape(cap, 4, 4, 8, 2, 4, BLK)

    def at(v, i, axis):
        return lax.dynamic_index_in_dim(v, i, axis=axis, keepdims=False)

    w_0 = at(w_tiles[:, :, :, :, 0], y, 4)
    w_1 = jnp.moveaxis(w_tiles[:, :, :, :, 1], 4, 0)
    halves = (2, 4, cap, 4, 8, BLK)
    pass_0 = jnp.moveaxis(at(w_0.reshape(cap, 2, 2, 4, 8, BLK), xl, 2), 1, 0)[:, None]
    pass_1 = jnp.moveaxis(at(w_1.reshape(4, cap, 2, 2, 4, 8, BLK), xl, 3), 2, 0)
    grad_0 = jnp.moveaxis(w_0, 1, 0)[None]
    grad_1 = at(w_1, y, 2)[None]
    to_shards = jnp.stack(
        [
            jnp.stack([jnp.broadcast_to(v, halves) for v in pair], axis=2)
            for pair in ((pass_0, pass_1), (grad_0, grad_1))
        ],
        axis=3,
    ).reshape(shards, 2 * cap * 4, 8, BLK)
    w_both = lax.all_to_all(to_shards, "shard", 0, 0, tiled=True)
    w_both = w_both.reshape(shards * 2 * cap, 32, BLK)
    at_slot = (block_slot >> 2) * (2 * cap) + (block_slot & 3)
    w_pass = [jnp.take(w_both, at_slot, axis=0, mode="clip")]
    w_rows = jnp.take(w_both, at_slot + cap, axis=0, mode="clip")
    w_pass += [send_on((X, X), w_pass[0], k) for k in SHIFTS]
    (w_b,) = small_kernel(_place_kernel, [(four_parts, BF)], [(x - lag) & 3], w_pass)
    w_b = w_b.reshape(width, BLK)
    w_own = [w_b] + [send_on(STAGE["a"], w_b, k) for k in (1, 3)]
    top = width // 2
    w_own.append(send_on(STAGE["a"], w_own[1][:top], 1))
    w_own.append(send_on(STAGE["a"], w_own[2][top:], 3))
    w_other = [send_core(p) for p in w_own]
    terms = small_kernel(
        _split_kernel,
        [((nblk, 32, BLK), BF)] * 4,
        [(me_b + lag) & 3],
        [t.reshape(-1, 4, 32, BLK) for t in terms],
    )
    terms = [terms[0]] + [send_on(STAGE["b"], terms[i + 1], k) for i, k in enumerate(SHIFTS)]

    projected, token_grad = token_work(
        order, tokens, inv_rms, gain_row, key_bias.reshape(1, kvw), cotangent, w_own + w_other
    )

    (to_owners,) = small_kernel(
        _owners_kernel,
        [((shards, cap * 32 + nblk + 16, BLK), BF)],
        [block_of_slot, me_b.reshape(1)],
        [*terms, w_rows, bias_rows],
        [pltpu.VMEM((nblk + 1, 32, BLK), BF)],
    )
    got = lax.all_to_all(to_owners, "shard", 0, 0, tiled=True)
    n_own = (shards // 2) * cap * 32
    message = ((n_own + 2 * (nblk + 8), BLK), BF)
    (mine,) = small_kernel(lambda *r: _group_kernel(nblk, *r), [message], [], [got])

    got = _send(mine, lambda x, y, z, c: (x ^ 1, y, z, c))
    (mine,) = small_kernel(lambda *r: _pair_kernel(n_own, *r), [message], [], [mine, got])
    got = [mine] + [send_on((Y, Y), mine, k) for k in SHIFTS]
    weight_grad, gain_grad, bias_grad = small_kernel(
        lambda *r: _finish_kernel(n_own, cap, *r),
        [((cap * BLK, kvw), F32), ((nblk, BLK), F32), ((8, BLK), F32)],
        [(y - lag) & 3],
        [*got, norm_gain.reshape(nblk, BLK)],
    )
    gain_grad = gain_grad.reshape(width)
    bias_grad = bias_grad.reshape(kvw)

    return (projected, token_grad, weight_grad, gain_grad, bias_grad)


def solution(mesh):
    return _mapped(mesh)


def _mapped(mesh):
    return jax.shard_map(
        local,
        mesh=mesh,
        in_specs=(
            P(("shard", "rep"), None),
            P(),
            P(),
            P("shard", None),
            P(("shard", "rep"), None),
            P(),
        ),
        out_specs=(
            P(("shard", "rep"), None),
            P(("shard", "rep"), None),
            P("shard", None),
            P(),
            P(),
        ),
        check_vma=False,
    )
```

profile of v0, /device:TPU:2, one launch (start us, length us, event | category | flops | bytes accessed | tf_op | source)
XLA Modules:
  0.0 178.7 jit_solution(3757667187257374338)
XLA Ops:
  0.7 1.3 fusion.5
  2.5 1.1 pad_maximum_fusion
  3.6 7.2 %all-to-all-start = ((bf16[16,32,8,128]{3,2,1,0:T(8,128)(2,1)}), bf16[16,32,8,128]{3,2,1,0:T(8,128)(2,1)S(1)}, u32[]{:S(2)}, u32[]{:S(2)}) async-start(bf16[16,32,8,128]{3,2,1,0:T(8,128)(2,1)} %bitcast.19), calls=%async_computation | async-start | bytes 2097152 | tf_op jit(solution)/shard_map/all_to_all | solution.py:385
  10.8 0.5 collective-permute-start.13
  11.3 3.0 %multiply_reduce_fusion = f32[384]{0:T(512)S(1)} fusion(bf16[384,5120]{1,0:T(8,128)(2,1)} %refs_5_.1), kind=kLoop, calls=%fused_computation.3 | loop fusion | flops 5897856 | bytes 3933696 | tf_op jit(solution)/shard_map/reduce_sum | solution.py:53
  14.3 14.5 %all-to-all-done = bf16[16,32,8,128]{3,2,1,0:T(8,128)(2,1)S(1)} async-done(((bf16[16,32,8,128]{3,2,1,0:T(8,128)(2,1)}), bf16[16,32,8,128]{3,2,1,0:T(8,128)(2,1)S(1)}, u32[]{:S(2)}, u32[]{:S(2)}) %all-to-all-start) | async-done | bytes 1048608 | tf_op jit(solution)/shard_map/all_to_all | solution.py:385
  28.8 0.6 gather_fusion
  29.5 0.3 copy-done.7
  29.8 0.1 rsqrt.7.inv.refs_1_
  30.1 0.5 and_add_fusion
  30.6 0.9 collective-permute-done.12.refs_2_
  31.5 0.7 copy-done.13
  32.2 0.3 copy-done.9
  32.4 11.0 %weight_terms.1 = (bf16[5120,128]{1,0:T(8,128)(2,1)}, bf16[2560,128]{1,0:T(8,128)(2,1)}, bf16[2560,128]{1,0:T(8,128)(2,1)}, bf16[2560,128]{1,0:T(8,128)(2,1)}, b...) custom-call(s32[4]{0:T(128)} %get-tuple-element.47.refs_0_, f32[384,1]{1,0:T(8,128)} %copy-done.3, ...), custom_call_target="tpu_custom_call" | custom-call | tf_op jit(solution)/shard_map/weight_terms/pallas_call | solution.py:117
  43.4 1.6 collective-permute-start.16
  45.0 1.7 collective-permute-start.17
  46.6 1.8 %collective-permute-start.15 = (bf16[2560,128]{1,0:T(8,128)(2,1)}, bf16[2560,128]{1,0:T(8,128)(2,1)}, u32[]{:S(2)}, u32[]{:S(2)}) collective-permute-start(bf16[2560,128]{1,0:T(8,128)(2,1)} %get-tuple-element.26), channel_id=1, source_target_pairs={{0,3},{8,56},{16,19},{24,8},{32,35},{40,24},{48,51},{56,40},{1,0},... | collective-permute-start | bytes 1966088 | tf_op jit(solution)/shard_map/ppermute | solution.py:36
  48.4 1.7 collective-permute-start.1
  50.1 1.5 collective-permute-start.2
  51.7 0.5 add_and_fusion
  52.2 6.0 %collective-permute-done.1.three = bf16[40,32,128]{2,1,0:T(8,128)(2,1)S(1)} collective-permute-done((bf16[40,32,128]{2,1,0:T(8,128)(2,1)S(1)}, bf16[40,32,128]{2,1,0:T(8,128)(2,1)S(1)}, u32[]{:S(2)}, u32[]{:S(2)}) %collective-permute-start.1) | collective-permute-done | bytes 327712 | tf_op jit(solution)/shard_map/ppermute | solution.py:36
  58.2 6.0 %collective-permute-done.2.four = bf16[40,32,128]{2,1,0:T(8,128)(2,1)S(1)} collective-permute-done((bf16[40,32,128]{2,1,0:T(8,128)(2,1)S(1)}, bf16[40,32,128]{2,1,0:T(8,128)(2,1)S(1)}, u32[]{:S(2)}, u32[]{:S(2)}) %collective-permute-start.2) | collective-permute-done | bytes 327712 | tf_op jit(solution)/shard_map/ppermute | solution.py:36
  64.3 0.7 copy-done.12
  65.0 2.4 %shard_map.110 = bf16[40,4,32,128]{3,2,1,0:T(8,128)(2,1)} custom-call(s32[4]{0:T(128)} %get-tuple-element.51.index, bf16[40,32,128]{2,1,0:T(8,128)(2,1)} %copy-done.8, bf16[40,32,128]{2,1,0:T(8,128)(2,1)} %copy-done.10, bf16[40,32,128]{2,1,0:T(8,128)(2,1)} %copy-done.11, bf16[40,32,128]{2,1,0:T(8,128)(2,1)} %copy-done.12), custom_call_target="tpu_custom_call" | custom-call | tf_op jit(solution)/shard_map/pallas_call | solution.py:201
  67.4 1.6 collective-permute-start.3
  69.0 1.6 collective-permute-start.19
  70.6 2.9 %shard_map.111 = (bf16[2560,128]{1,0:T(8,128)(2,1)}, bf16[2560,128]{1,0:T(8,128)(2,1)}) custom-call(bf16[2560,128]{1,0:T(8,128)(2,1)} %get-tuple-element.27.one, bf16[2560,128]{1,0:T(8,128)(2,1)} %collective-permute-done.16.two, bf16[2560,128]{1,0:T(8,128)(2,1)} %get-tuple-element.29.three, bf16[2560,128]{1,0:T(8,128)(2,1)} %collective-permute-done.17.four), custom_call_target="tpu_custom_call" | custom-call | tf_op jit(solution)/shard_map/pallas_call | solution.py:201
  73.5 1.3 collective-permute-start.18
  74.8 2.0 %collective-permute-start.20 = (bf16[2560,128]{1,0:T(8,128)(2,1)}, bf16[2560,128]{1,0:T(8,128)(2,1)}, u32[]{:S(2)}, u32[]{:S(2)}) collective-permute-start(bf16[2560,128]{1,0:T(8,128)(2,1)} %get-tuple-element.33), channel_id=1, source_target_pairs={{0,3},{8,56},{16,19},{24,8},{32,35},{40,24},{48,51},{56,40},{1,0},... | collective-permute-start | bytes 1966088 | tf_op jit(solution)/shard_map/ppermute | solution.py:36
  76.8 0.4 collective-permute-start.4
  77.2 1.2 scatter_custom_fusion.block_of_slot
  78.4 0.1 convert_reduce_fusion
  78.5 15.0 %collective-permute-done.19 = bf16[2560,128]{1,0:T(8,128)(2,1)} collective-permute-done((bf16[2560,128]{1,0:T(8,128)(2,1)}, bf16[2560,128]{1,0:T(8,128)(2,1)}, u32[]{:S(2)}, u32[]{:S(2)}) %collective-permute-start.19) | collective-permute-done | bytes 655392 | tf_op jit(solution)/shard_map/ppermute | solution.py:36
  93.6 7.0 %collective-permute-done.18 = bf16[2560,128]{1,0:T(8,128)(2,1)} collective-permute-done((bf16[2560,128]{1,0:T(8,128)(2,1)}, bf16[2560,128]{1,0:T(8,128)(2,1)}, u32[]{:S(2)}, u32[]{:S(2)}) %collective-permute-start.18) | collective-permute-done | bytes 655392 | tf_op jit(solution)/shard_map/ppermute | solution.py:36
  100.6 3.5 %shard_map.112 = (bf16[40,32,128]{2,1,0:T(8,128)(2,1)}, bf16[40,32,128]{2,1,0:T(8,128)(2,1)}, bf16[40,32,128]{2,1,0:T(8,128)(2,1)}, bf16[40,32,128]{2,1,0:T(8,128)(2,1)}) custom-call(s32[4]{0:T(128)} %get-tuple-element.48.index, bf16[40,4,32,128]{3,2,1,0:T(8,128)(2,1)} %bitcast.60, bf16[20,4,32,128]{3,2,1,0:T(8,128)(2,1)} %bitcast.24.top_1, ...), custom_call_target="tpu_custom_call" | custom-call | tf_op jit(solution)/shard_map/pallas_call | solution.py:201
  104.1 1.5 collective-permute-start.21
  105.6 1.7 collective-permute-start.22
  107.4 0.3 collective-permute-start.23
  107.7 0.6 pad_maximum_fusion.1.bias
  108.3 2.6 %gather_fusion.1 = bf16[40,32,128]{2,1,0:T(8,128)(2,1)} fusion(bf16[128,32,128]{2,1,0:T(8,128)(2,1)} %bitcast.58, s32[1024]{0:T(1024)S(1)} %pad_clamp_fusion), kind=kCustom, calls=%fused_computation.1 | custom fusion | bytes 655520 | tf_op jit(solution)/shard_map/jit(_take)/gather | solution.py:389
  110.9 1.9 %collective-permute-done.21.two = bf16[40,32,128]{2,1,0:T(8,128)(2,1)} collective-permute-done((bf16[40,32,128]{2,1,0:T(8,128)(2,1)}, bf16[40,32,128]{2,1,0:T(8,128)(2,1)}, u32[]{:S(2)}, u32[]{:S(2)}) %collective-permute-start.21) | collective-permute-done | bytes 327712 | tf_op jit(solution)/shard_map/ppermute | solution.py:36
  112.7 0.3 collective-permute-done.22.three
  113.0 3.2 %collective-permute-done.23.four = bf16[40,32,128]{2,1,0:T(8,128)(2,1)} collective-permute-done((bf16[40,32,128]{2,1,0:T(8,128)(2,1)}, bf16[40,32,128]{2,1,0:T(8,128)(2,1)}, u32[]{:S(2)}, u32[]{:S(2)}) %collective-permute-start.23) | collective-permute-done | bytes 327712 | tf_op jit(solution)/shard_map/ppermute | solution.py:36
  116.3 2.6 %shard_map.113 = bf16[16,184,128]{2,1,0:T(8,128)(2,1)} custom-call(s32[64]{0:T(128)} %scatter_custom_fusion.block_of_slot, s32[1]{0:T(128)} %bitcast.22.row_block, bf16[40,32,128]{2,1,0:T(8,128)(2,1)} %get-tuple-element.34.one, bf16[40,32,128]{2,1,0:T(8,128)(2,1)} %collective-permute-done.21.two, bf16[40,32,128]{2,1,0:T(8,128)(2,1)} %collective-permute-done.22.three, ...), custom_call_target="tpu_custom_call" | custom-call | tf_op jit(solution)/shard_map/pallas_call | solution.py:201
  118.9 7.2 %all-to-all-start.1 = ((bf16[16,184,128]{2,1,0:T(8,128)(2,1)}), bf16[16,184,128]{2,1,0:T(8,128)(2,1)}, u32[]{:S(2)}, u32[]{:S(2)}) async-start(bf16[16,184,128]{2,1,0:T(8,128)(2,1)} %shard_map.113), calls=%async_computation.1 | async-start | bytes 1507328 | tf_op jit(solution)/shard_map/all_to_all | solution.py:417
  126.0 0.9 slice.22
  126.9 0.4 collective-permute-start.5
  127.3 1.3 collective-permute-start.7
  128.6 2.0 %slice.23 = bf16[2560,128]{1,0:T(8,128)(2,1)} slice(bf16[5120,128]{1,0:T(8,128)(2,1)} %collective-permute-done.4.rest_2_), slice={[2560:5120], [0:128]} | slice | bytes 1310720 | tf_op jit(solution)/shard_map/slice | solution.py:396
  130.6 1.8 %collective-permute-start.6 = (bf16[2560,128]{1,0:T(8,128)(2,1)}, bf16[2560,128]{1,0:T(8,128)(2,1)}, u32[]{:S(2)}, u32[]{:S(2)}) collective-permute-start(bf16[2560,128]{1,0:T(8,128)(2,1)} %slice.23), channel_id=1, source_target_pairs={{0,3},{8,56},{16,19},{24,8},{32,35},{40,24},{48,51},{56,40},{1,0},... | collective-permute-start | bytes 1966088 | tf_op jit(solution)/shard_map/ppermute | solution.py:36
  132.4 0.2 collective-permute-start.8
  132.6 0.3 collective-permute-start.9
  132.9 8.0 %all-to-all-done.1.r_0_ = bf16[16,184,128]{2,1,0:T(8,128)(2,1)} async-done(((bf16[16,184,128]{2,1,0:T(8,128)(2,1)}), bf16[16,184,128]{2,1,0:T(8,128)(2,1)}, u32[]{:S(2)}, u32[]{:S(2)}) %all-to-all-start.1) | async-done | bytes 753696 | tf_op jit(solution)/shard_map/all_to_all | solution.py:417
  140.9 1.9 %shard_map.114.r_0_ = bf16[1120,128]{1,0:T(8,128)(2,1)} custom-call(bf16[16,184,128]{2,1,0:T(8,128)(2,1)} %all-to-all-done.1.r_0_), custom_call_target="tpu_custom_call" | custom-call | tf_op jit(solution)/shard_map/pallas_call | solution.py:201
  142.9 2.5 %collective-permute-start.10 = (bf16[2560,128]{1,0:T(8,128)(2,1)}, bf16[2560,128]{1,0:T(8,128)(2,1)}, u32[]{:S(2)}, u32[]{:S(2)}) collective-permute-start(bf16[2560,128]{1,0:T(8,128)(2,1)} %collective-permute-done.5.rest_3_), channel_id=1, source_target_pairs={{0,8},{8,0},{16,24},{24,16},{32,40},{40,32},{48,56},{56,48},{1,9},... | collective-permute-start | bytes 1966088 | tf_op jit(solution)/shard_map/ppermute | solution.py:36
  145.3 6.1 %collective-permute-done.24.r_1_ = bf16[1120,128]{1,0:T(8,128)(2,1)} collective-permute-done((bf16[1120,128]{1,0:T(8,128)(2,1)}, bf16[1120,128]{1,0:T(8,128)(2,1)}, u32[]{:S(2)}, u32[]{:S(2)}) %collective-permute-start.24) | collective-permute-done | bytes 286752 | tf_op jit(solution)/shard_map/ppermute | solution.py:36
  151.4 1.3 collective-permute-start.11
  152.7 1.8 %shard_map.115.r_1_ = bf16[1120,128]{1,0:T(8,128)(2,1)} custom-call(bf16[1120,128]{1,0:T(8,128)(2,1)} %shard_map.114.r_0_, bf16[1120,128]{1,0:T(8,128)(2,1)} %collective-permute-done.24.r_1_), custom_call_target="tpu_custom_call" | custom-call | tf_op jit(solution)/shard_map/pallas_call | solution.py:201
  154.5 0.4 collective-permute-start.25
  154.9 2.9 %collective-permute-start.26 = (bf16[1120,128]{1,0:T(8,128)(2,1)}, bf16[1120,128]{1,0:T(8,128)(2,1)}, u32[]{:S(2)}, u32[]{:S(2)}) collective-permute-start(bf16[1120,128]{1,0:T(8,128)(2,1)} %shard_map.115.r_1_), channel_id=1, source_target_pairs={{0,3},{8,11},{16,19},{24,27},{32,35},{40,43},{48,51},{56,59},{1,0}... | collective-permute-start | bytes 860168 | tf_op jit(solution)/shard_map/ppermute | solution.py:36
  157.8 0.8 collective-permute-start.27
  158.7 0.9 copy-done.4
  159.6 16.3 %token_work.1 = (bf16[384,1024]{1,0:T(8,128)(2,1)}, bf16[384,5120]{1,0:T(8,128)(2,1)}) custom-call(s32[8]{0:T(128)S(1)} %pad_add_fusion.tiles, bf16[384,5120]{1,0:T(8,128)(2,1)} %refs_5_.1, f32[384,1]{1,0:T(8,128)S(1)} %copy-done.4, f32[1,5120]{1,0:T(1,128)S(1)} %bitcast.55, f32[1,1024]{1,0:T(1,128)S(1)} %bitcast.56, bf16[384,1024]{1,0:T(8,128)(2,1)S(1)} %copy-done.1, ...), custom_call_target="tpu_custom_call" | custom-call | tf_op jit(solution)/shard_map/token_work/pallas_call | solution.py:177
  175.9 2.8 %shard_map.116 = (f32[512,1024]{1,0:T(8,128)}, f32[40,128]{1,0:T(8,128)}, f32[8,128]{1,0:T(8,128)}) custom-call(s32[4]{0:T(128)} %get-tuple-element.50.r_0_, bf16[1120,128]{1,0:T(8,128)(2,1)} %shard_map.115.r_1_, bf16[1120,128]{1,0:T(8,128)(2,1)} %collective-permute-done.25.r_2_, bf16[1120,128]{1,0:T(8,128)(2,1)} %collective-permute-done.26.r_3_, ...), custom_call_target="tpu_custom_call" | custom-call | tf_op jit(solution)/shard_map/pallas_call | solution.py:201
  (69 shorter events, 0.8 us)
Async XLA Ops:
  0.6 30.9 %collective-permute-start.14 = (bf16[384,5120]{1,0:T(8,128)(2,1)}, bf16[384,5120]{1,0:T(8,128)(2,1)}, u32[]{:S(2)}, u32[]{:S(2)}) collective-permute-start(bf16[384,5120]{1,0:T(8,128)(2,1)} %refs_5_.1), channel_id=1, source_target_pairs={{0,8},{8,0},{16,24},{24,16},{32,40},{40,32},{48,56},{56,48},{1,9},... | collective-permute-start | bytes 11796488 | tf_op jit(solution)/shard_map/ppermute | solution.py:36
  3.6 7.2 %copy-start = (bf16[384,1024]{1,0:T(8,128)(2,1)S(1)}, bf16[384,1024]{1,0:T(8,128)(2,1)}, u32[]{:S(2)}) copy-start(bf16[384,1024]{1,0:T(8,128)(2,1)} %refs_3_.1) | copy-start | bytes 2359300
  3.6 7.7 %copy-start.14 = (s32[40]{0:T(128)S(1)}, s32[40]{0:T(128)}, u32[]{:S(2)}) copy-start(s32[40]{0:T(128)} %param.12) | copy-start | bytes 484
  3.6 25.2 %all-to-all-start = ((bf16[16,32,8,128]{3,2,1,0:T(8,128)(2,1)}), bf16[16,32,8,128]{3,2,1,0:T(8,128)(2,1)S(1)}, u32[]{:S(2)}, u32[]{:S(2)}) async-start(bf16[16,32,8,128]{3,2,1,0:T(8,128)(2,1)} %bitcast.19), calls=%async_computation | async-start | bytes 2097152 | tf_op jit(solution)/shard_map/all_to_all | solution.py:385
  10.8 20.7 %collective-permute-start.13 = (bf16[384,1024]{1,0:T(8,128)(2,1)S(1)}, bf16[384,1024]{1,0:T(8,128)(2,1)S(1)}, u32[]{:S(2)}, u32[]{:S(2)}) collective-permute-start(bf16[384,1024]{1,0:T(8,128)(2,1)S(1)} %copy-done), channel_id=1, source_target_pairs={{0,8},{8,0},{16,24},{24,16},{32,40},{40,32},{48,56},{56,48},{1,9},... | collective-permute-start | bytes 2359304 | tf_op jit(solution)/shard_map/ppermute | solution.py:36
  11.3 18.8 %copy-start.15 = (s32[4]{0:T(128)S(1)}, s32[4]{0:T(128)}, u32[]{:S(2)}) copy-start(s32[4]{0:T(128)} %constant.59.clone) | copy-start | bytes 52
  28.8 1.0 copy-start.7
  29.4 20.7 %copy-start.8 = (bf16[40,32,128]{2,1,0:T(8,128)(2,1)}, bf16[40,32,128]{2,1,0:T(8,128)(2,1)S(1)}, u32[]{:S(2)}) copy-start(bf16[40,32,128]{2,1,0:T(8,128)(2,1)S(1)} %gather_fusion) | copy-start | bytes 983044
  29.4 20.7 %collective-permute-start = (bf16[40,32,128]{2,1,0:T(8,128)(2,1)S(1)}, bf16[40,32,128]{2,1,0:T(8,128)(2,1)S(1)}, u32[]{:S(2)}, u32[]{:S(2)}) collective-permute-start(bf16[40,32,128]{2,1,0:T(8,128)(2,1)S(1)} %gather_fusion), channel_id=1, source_target_pairs={{0,4},{8,12},{16,20},{24,28},{32,36},{40,44},{48,52},{56,60},{1,5}... | collective-permute-start | bytes 983048 | tf_op jit(solution)/shard_map/ppermute | solution.py:36
  30.0 1.5 copy-start.3
  30.0 1.5 collective-permute-start.12
  31.5 0.7 copy-start.13
  31.5 0.9 copy-start.9
  32.4 19.2 %copy-start.16 = (s32[4]{0:T(128)S(1)}, s32[4]{0:T(128)}, u32[]{:S(2)}) copy-start(s32[4]{0:T(128)} %constant.60) | copy-start | bytes 52
  43.4 27.2 %collective-permute-start.16 = (bf16[2560,128]{1,0:T(8,128)(2,1)}, bf16[2560,128]{1,0:T(8,128)(2,1)}, u32[]{:S(2)}, u32[]{:S(2)}) collective-permute-start(bf16[2560,128]{1,0:T(8,128)(2,1)} %get-tuple-element.28), channel_id=1, source_target_pairs={{0,1},{8,24},{16,17},{24,40},{32,33},{40,56},{48,49},{56,8},{1,2},... | collective-permute-start | bytes 1966088 | tf_op jit(solution)/shard_map/ppermute | solution.py:36
  45.0 25.6 %collective-permute-start.17 = (bf16[2560,128]{1,0:T(8,128)(2,1)}, bf16[2560,128]{1,0:T(8,128)(2,1)}, u32[]{:S(2)}, u32[]{:S(2)}) collective-permute-start(bf16[2560,128]{1,0:T(8,128)(2,1)} %get-tuple-element.30), channel_id=1, source_target_pairs={{0,3},{8,56},{16,19},{24,8},{32,35},{40,24},{48,51},{56,40},{1,0},... | collective-permute-start | bytes 1966088 | tf_op jit(solution)/shard_map/ppermute | solution.py:36
  46.6 30.1 %collective-permute-start.15 = (bf16[2560,128]{1,0:T(8,128)(2,1)}, bf16[2560,128]{1,0:T(8,128)(2,1)}, u32[]{:S(2)}, u32[]{:S(2)}) collective-permute-start(bf16[2560,128]{1,0:T(8,128)(2,1)} %get-tuple-element.26), channel_id=1, source_target_pairs={{0,3},{8,56},{16,19},{24,8},{32,35},{40,24},{48,51},{56,40},{1,0},... | collective-permute-start | bytes 1966088 | tf_op jit(solution)/shard_map/ppermute | solution.py:36
  48.4 9.8 %collective-permute-start.1 = (bf16[40,32,128]{2,1,0:T(8,128)(2,1)S(1)}, bf16[40,32,128]{2,1,0:T(8,128)(2,1)S(1)}, u32[]{:S(2)}, u32[]{:S(2)}) collective-permute-start(bf16[40,32,128]{2,1,0:T(8,128)(2,1)S(1)} %gather_fusion), channel_id=1, source_target_pairs={{0,68},{8,76},{16,84},{24,92},{32,100},{40,108},{48,116},{56,124},... | collective-permute-start | bytes 983048 | tf_op jit(solution)/shard_map/ppermute | solution.py:36
  50.1 14.1 %copy-start.10 = (bf16[40,32,128]{2,1,0:T(8,128)(2,1)}, bf16[40,32,128]{2,1,0:T(8,128)(2,1)S(1)}, u32[]{:S(2)}) copy-start(bf16[40,32,128]{2,1,0:T(8,128)(2,1)S(1)} %collective-permute-done.two) | copy-start | bytes 983044
  50.1 14.1 %collective-permute-start.2 = (bf16[40,32,128]{2,1,0:T(8,128)(2,1)S(1)}, bf16[40,32,128]{2,1,0:T(8,128)(2,1)S(1)}, u32[]{:S(2)}, u32[]{:S(2)}) collective-permute-start(bf16[40,32,128]{2,1,0:T(8,128)(2,1)S(1)} %gather_fusion), channel_id=1, source_target_pairs={{0,64},{8,72},{16,80},{24,88},{32,96},{40,104},{48,112},{56,120},{... | collective-permute-start | bytes 983048 | tf_op jit(solution)/shard_map/ppermute | solution.py:36
  58.2 6.0 %copy-start.11 = (bf16[40,32,128]{2,1,0:T(8,128)(2,1)}, bf16[40,32,128]{2,1,0:T(8,128)(2,1)S(1)}, u32[]{:S(2)}) copy-start(bf16[40,32,128]{2,1,0:T(8,128)(2,1)S(1)} %collective-permute-done.1.three) | copy-start | bytes 983044
  64.3 0.7 copy-start.12
  67.4 9.3 %copy-start.2 = (bf16[40,4,32,128]{3,2,1,0:T(8,128)(2,1)S(1)}, bf16[40,4,32,128]{3,2,1,0:T(8,128)(2,1)}, u32[]{:S(2)}) copy-start(bf16[40,4,32,128]{3,2,1,0:T(8,128)(2,1)} %shard_map.110) | copy-start | bytes 3932164
  67.4 11.0 %copy-start.1 = (bf16[384,1024]{1,0:T(8,128)(2,1)S(1)}, bf16[384,1024]{1,0:T(8,128)(2,1)}, u32[]{:S(2)}) copy-start(bf16[384,1024]{1,0:T(8,128)(2,1)} %refs_3_.1) | copy-start | bytes 2359300
  67.4 58.6 %collective-permute-start.3 = (bf16[5120,128]{1,0:T(8,128)(2,1)}, bf16[5120,128]{1,0:T(8,128)(2,1)S(1)}, u32[]{:S(2)}, u32[]{:S(2)}) collective-permute-start(bf16[5120,128]{1,0:T(8,128)(2,1)} %bitcast.49), channel_id=1, source_target_pairs={{0,1},{8,24},{16,17},{24,40},{32,33},{40,56},{48,49},{56,8},{1,2},... | collective-permute-start | bytes 3932168 | tf_op jit(solution)/shard_map/ppermute | solution.py:36
  69.0 24.6 %collective-permute-start.19 = (bf16[2560,128]{1,0:T(8,128)(2,1)}, bf16[2560,128]{1,0:T(8,128)(2,1)}, u32[]{:S(2)}, u32[]{:S(2)}) collective-permute-start(bf16[2560,128]{1,0:T(8,128)(2,1)} %get-tuple-element.32), channel_id=1, source_target_pairs={{0,1},{8,24},{16,17},{24,40},{32,33},{40,56},{48,49},{56,8},{1,2},... | collective-permute-start | bytes 1966088 | tf_op jit(solution)/shard_map/ppermute | solution.py:36
  73.5 27.1 %collective-permute-start.18 = (bf16[2560,128]{1,0:T(8,128)(2,1)}, bf16[2560,128]{1,0:T(8,128)(2,1)}, u32[]{:S(2)}, u32[]{:S(2)}) collective-permute-start(bf16[2560,128]{1,0:T(8,128)(2,1)} %get-tuple-element.31), channel_id=1, source_target_pairs={{0,1},{8,24},{16,17},{24,40},{32,33},{40,56},{48,49},{56,8},{1,2},... | collective-permute-start | bytes 1966088 | tf_op jit(solution)/shard_map/ppermute | solution.py:36
  74.8 25.8 %collective-permute-start.20 = (bf16[2560,128]{1,0:T(8,128)(2,1)}, bf16[2560,128]{1,0:T(8,128)(2,1)}, u32[]{:S(2)}, u32[]{:S(2)}) collective-permute-start(bf16[2560,128]{1,0:T(8,128)(2,1)} %get-tuple-element.33), channel_id=1, source_target_pairs={{0,3},{8,56},{16,19},{24,8},{32,35},{40,24},{48,51},{56,40},{1,0},... | collective-permute-start | bytes 1966088 | tf_op jit(solution)/shard_map/ppermute | solution.py:36
  76.8 51.9 %collective-permute-start.4 = (bf16[5120,128]{1,0:T(8,128)(2,1)S(1)}, bf16[5120,128]{1,0:T(8,128)(2,1)}, u32[]{:S(2)}, u32[]{:S(2)}) collective-permute-start(bf16[5120,128]{1,0:T(8,128)(2,1)S(1)} %bitcast.50), channel_id=1, source_target_pairs={{0,3},{8,56},{16,19},{24,8},{32,35},{40,24},{48,51},{56,40},{1,0},... | collective-permute-start | bytes 3932168 | tf_op jit(solution)/shard_map/ppermute | solution.py:36
  104.1 8.6 %collective-permute-start.21 = (bf16[40,32,128]{2,1,0:T(8,128)(2,1)}, bf16[40,32,128]{2,1,0:T(8,128)(2,1)}, u32[]{:S(2)}, u32[]{:S(2)}) collective-permute-start(bf16[40,32,128]{2,1,0:T(8,128)(2,1)} %get-tuple-element.35), channel_id=1, source_target_pairs={{0,16},{8,9},{16,32},{24,25},{32,48},{40,41},{48,0},{56,57},{1,17}... | collective-permute-start | bytes 983048 | tf_op jit(solution)/shard_map/ppermute | solution.py:36
  105.6 7.4 %collective-permute-start.22 = (bf16[40,32,128]{2,1,0:T(8,128)(2,1)}, bf16[40,32,128]{2,1,0:T(8,128)(2,1)}, u32[]{:S(2)}, u32[]{:S(2)}) collective-permute-start(bf16[40,32,128]{2,1,0:T(8,128)(2,1)} %get-tuple-element.36), channel_id=1, source_target_pairs={{0,48},{8,11},{16,0},{24,27},{32,16},{40,43},{48,32},{56,59},{1,49... | collective-permute-start | bytes 983048 | tf_op jit(solution)/shard_map/ppermute | solution.py:36
  107.4 8.9 %collective-permute-start.23 = (bf16[40,32,128]{2,1,0:T(8,128)(2,1)}, bf16[40,32,128]{2,1,0:T(8,128)(2,1)}, u32[]{:S(2)}, u32[]{:S(2)}) collective-permute-start(bf16[40,32,128]{2,1,0:T(8,128)(2,1)} %get-tuple-element.37), channel_id=1, source_target_pairs={{0,32},{8,10},{16,48},{24,26},{32,0},{40,42},{48,16},{56,58},{1,33... | collective-permute-start | bytes 983048 | tf_op jit(solution)/shard_map/ppermute | solution.py:36
  118.9 22.1 %all-to-all-start.1 = ((bf16[16,184,128]{2,1,0:T(8,128)(2,1)}), bf16[16,184,128]{2,1,0:T(8,128)(2,1)}, u32[]{:S(2)}, u32[]{:S(2)}) async-start(bf16[16,184,128]{2,1,0:T(8,128)(2,1)} %shard_map.113), calls=%async_computation.1 | async-start | bytes 1507328 | tf_op jit(solution)/shard_map/all_to_all | solution.py:417
  126.9 31.7 %copy-start.5 = (f32[5120]{0:T(1024)S(1)}, f32[5120]{0:T(1024)}, u32[]{:S(2)}) copy-start(f32[5120]{0:T(1024)} %param.8) | copy-start | bytes 61444
  126.9 31.7 %copy-start.6 = (f32[1024]{0:T(1024)S(1)}, f32[1024]{0:T(1024)}, u32[]{:S(2)}) copy-start(f32[1024]{0:T(1024)} %param.9) | copy-start | bytes 12292
  126.9 15.9 %collective-permute-start.5 = (bf16[2560,128]{1,0:T(8,128)(2,1)}, bf16[2560,128]{1,0:T(8,128)(2,1)}, u32[]{:S(2)}, u32[]{:S(2)}) collective-permute-start(bf16[2560,128]{1,0:T(8,128)(2,1)} %slice.22), channel_id=1, source_target_pairs={{0,1},{8,24},{16,17},{24,40},{32,33},{40,56},{48,49},{56,8},{1,2},... | collective-permute-start | bytes 1966088 | tf_op jit(solution)/shard_map/ppermute | solution.py:36
  127.3 27.3 %collective-permute-start.7 = (bf16[5120,128]{1,0:T(8,128)(2,1)S(1)}, bf16[5120,128]{1,0:T(8,128)(2,1)}, u32[]{:S(2)}, u32[]{:S(2)}) collective-permute-start(bf16[5120,128]{1,0:T(8,128)(2,1)S(1)} %bitcast.51), channel_id=1, source_target_pairs={{0,8},{8,0},{16,24},{24,16},{32,40},{40,32},{48,56},{56,48},{1,9},... | collective-permute-start | bytes 3932168 | tf_op jit(solution)/shard_map/ppermute | solution.py:36
  130.6 12.3 %collective-permute-start.6 = (bf16[2560,128]{1,0:T(8,128)(2,1)}, bf16[2560,128]{1,0:T(8,128)(2,1)}, u32[]{:S(2)}, u32[]{:S(2)}) collective-permute-start(bf16[2560,128]{1,0:T(8,128)(2,1)} %slice.23), channel_id=1, source_target_pairs={{0,3},{8,56},{16,19},{24,8},{32,35},{40,24},{48,51},{56,40},{1,0},... | collective-permute-start | bytes 1966088 | tf_op jit(solution)/shard_map/ppermute | solution.py:36
  132.4 26.2 %collective-permute-start.8 = (bf16[5120,128]{1,0:T(8,128)(2,1)S(1)}, bf16[5120,128]{1,0:T(8,128)(2,1)}, u32[]{:S(2)}, u32[]{:S(2)}) collective-permute-start(bf16[5120,128]{1,0:T(8,128)(2,1)S(1)} %collective-permute-done.3.rest_1_), channel_id=1, source_target_pairs={{0,8},{8,0},{16,24},{24,16},{32,40},{40,32},{48,56},{56,48},{1,9},... | collective-permute-start | bytes 3932168 | tf_op jit(solution)/shard_map/ppermute | solution.py:36
  132.6 26.1 %collective-permute-start.9 = (bf16[5120,128]{1,0:T(8,128)(2,1)}, bf16[5120,128]{1,0:T(8,128)(2,1)}, u32[]{:S(2)}, u32[]{:S(2)}) collective-permute-start(bf16[5120,128]{1,0:T(8,128)(2,1)} %collective-permute-done.4.rest_2_), channel_id=1, source_target_pairs={{0,8},{8,0},{16,24},{24,16},{32,40},{40,32},{48,56},{56,48},{1,9},... | collective-permute-start | bytes 3932168 | tf_op jit(solution)/shard_map/ppermute | solution.py:36
  142.8 8.5 %collective-permute-start.24 = (bf16[1120,128]{1,0:T(8,128)(2,1)}, bf16[1120,128]{1,0:T(8,128)(2,1)}, u32[]{:S(2)}, u32[]{:S(2)}) collective-permute-start(bf16[1120,128]{1,0:T(8,128)(2,1)} %shard_map.114.r_0_), channel_id=1, source_target_pairs={{0,4},{8,12},{16,20},{24,28},{32,36},{40,44},{48,52},{56,60},{1,5}... | collective-permute-start | bytes 860168 | tf_op jit(solution)/shard_map/ppermute | solution.py:36
  142.9 12.1 %collective-permute-start.10 = (bf16[2560,128]{1,0:T(8,128)(2,1)}, bf16[2560,128]{1,0:T(8,128)(2,1)}, u32[]{:S(2)}, u32[]{:S(2)}) collective-permute-start(bf16[2560,128]{1,0:T(8,128)(2,1)} %collective-permute-done.5.rest_3_), channel_id=1, source_target_pairs={{0,8},{8,0},{16,24},{24,16},{32,40},{40,32},{48,56},{56,48},{1,9},... | collective-permute-start | bytes 1966088 | tf_op jit(solution)/shard_map/ppermute | solution.py:36
  151.4 6.4 %collective-permute-start.11 = (bf16[2560,128]{1,0:T(8,128)(2,1)}, bf16[2560,128]{1,0:T(8,128)(2,1)}, u32[]{:S(2)}, u32[]{:S(2)}) collective-permute-start(bf16[2560,128]{1,0:T(8,128)(2,1)} %collective-permute-done.6.rest_4_), channel_id=1, source_target_pairs={{0,8},{8,0},{16,24},{24,16},{32,40},{40,32},{48,56},{56,48},{1,9},... | collective-permute-start | bytes 1966088 | tf_op jit(solution)/shard_map/ppermute | solution.py:36
  154.5 21.3 %collective-permute-start.25 = (bf16[1120,128]{1,0:T(8,128)(2,1)}, bf16[1120,128]{1,0:T(8,128)(2,1)}, u32[]{:S(2)}, u32[]{:S(2)}) collective-permute-start(bf16[1120,128]{1,0:T(8,128)(2,1)} %shard_map.115.r_1_), channel_id=1, source_target_pairs={{0,1},{8,9},{16,17},{24,25},{32,33},{40,41},{48,49},{56,57},{1,2},... | collective-permute-start | bytes 860168 | tf_op jit(solution)/shard_map/ppermute | solution.py:36
  154.9 21.0 %collective-permute-start.26 = (bf16[1120,128]{1,0:T(8,128)(2,1)}, bf16[1120,128]{1,0:T(8,128)(2,1)}, u32[]{:S(2)}, u32[]{:S(2)}) collective-permute-start(bf16[1120,128]{1,0:T(8,128)(2,1)} %shard_map.115.r_1_), channel_id=1, source_target_pairs={{0,3},{8,11},{16,19},{24,27},{32,35},{40,43},{48,51},{56,59},{1,0}... | collective-permute-start | bytes 860168 | tf_op jit(solution)/shard_map/ppermute | solution.py:36
  157.8 18.1 %collective-permute-start.27 = (bf16[1120,128]{1,0:T(8,128)(2,1)}, bf16[1120,128]{1,0:T(8,128)(2,1)}, u32[]{:S(2)}, u32[]{:S(2)}) collective-permute-start(bf16[1120,128]{1,0:T(8,128)(2,1)} %shard_map.115.r_1_), channel_id=1, source_target_pairs={{0,2},{8,10},{16,18},{24,26},{32,34},{40,42},{48,50},{56,58},{1,3}... | collective-permute-start | bytes 860168 | tf_op jit(solution)/shard_map/ppermute | solution.py:36
  158.7 0.9 copy-start.4
where the time goes:
time: 179 us
  waiting for transfers between devices  69 us (39%)
  starting transfers between devices  45.6 us (25%)
  Pallas kernels  45.2 us (25%)
  local copies, waits for them, and re-layouts  11.8 us (7%)
  other arithmetic  6.03 us (3%)
    ppermute x28, waiting for transfers between devices, _send(): return lax.ppermute(v, AXES, _pairs(move))  46.5 us
    ppermute x28, starting transfers between devices, _send(): return lax.ppermute(v, AXES, _pairs(move))  31.2 us
    pallas_call x7, Pallas kernels, small_kernel(): pl.pallas_call(body, in_specs=[smem] * len(scalars) + [vmem] * len(arrays...  18 us
    pallas_call x1, Pallas kernels, token_work(): pl.pallas_call(_tokens_kernel, in_specs=[pl.BlockSpec(memory_space=pltpu....  16.3 us
    all_to_all x1, waiting for transfers between devices, local(): w_both = lax.all_to_all(to_shards, 'shard', 0, 0, tiled=True)  14.5 us
    pallas_call x1, Pallas kernels, weight_terms(): pl.pallas_call(lambda *refs: _terms_kernel(scale, *refs), in_specs=[pl.Bl...  11 us
    all_to_all x1, waiting for transfers between devices, local(): got = lax.all_to_all(to_owners, 'shard', 0, 0, tiled=True)  7.99 us
    all_to_all x1, starting transfers between devices, local(): w_both = lax.all_to_all(to_shards, 'shard', 0, 0, tiled=True)  7.2 us
  transfers between devices with their start and end apart: 30, of which 11 were waited for; matrix products, arithmetic and copies ran while one was open for 8% of the time, Pallas kernels for 24%

commit v1 on v0

--- a/solution.py
+++ b/solution.py
@@ -128,30 +128,40 @@
 
 def _tokens_kernel(tiles, tok, inv, gain, bias, cot, *rest):
     pieces, (proj, grad) = rest[:10], rest[10:12]
-    turned, weight, acc, scaled, out, sems = rest[12:]
+    turned, weight, acc, scaled, out, sems, loads = rest[12:]
     _, width = tok.shape
     chunks = width // CHUNK
+    pulls = []
+    for j in range(chunks):
+        half = chunks // 2 * CHUNK
+        for i in range(8):
+            first = 5 * (i // 4) + i % 4
+            lower = i % 4 == 3 and j >= chunks // 2
+            start = j * CHUNK - (half if lower else 0)
+            pulls.append(
+                pltpu.make_async_copy(
+                    pieces[first + lower].at[start : start + CHUNK],
+                    weight.at[j, :, i * BLK : (i + 1) * BLK],
+                    loads.at[j, i],
+                )
+            )
+            pulls[-1].start()
     for i in range(8):
         turned[:, i * BLK : (i + 1) * BLK] = cot[:, _cols(tiles[i])]
     r = inv[...]
     for j in range(chunks):
         at = slice(j * CHUNK, (j + 1) * CHUNK)
-        for i in range(8):
-            first = 5 * (i // 4) + i % 4
-            piece, rows_at = pieces[first], at
-            if i % 4 == 3 and j >= chunks // 2:
-                half = chunks // 2 * CHUNK
-                piece, rows_at = pieces[first + 1], slice(at.start - half, at.stop - half)
-            weight[:, i * BLK : (i + 1) * BLK] = piece[rows_at]
+        for pull in pulls[8 * j : 8 * j + 8]:
+            pull.wait()
         g = gain[:, at]
         normed = (tok[:, at].astype(F32) * r * g).astype(BF)
-        part = jnp.dot(normed, weight[...], preferred_element_type=F32)
+        part = jnp.dot(normed, weight[j], preferred_element_type=F32)
         if j == 0:
             acc[...] = part
         else:
             acc[...] += part
         grad_normed = lax.dot_general(
-            turned[...], weight[...], (((1,), (1,)), ((), ())), preferred_element_type=F32
+            turned[...], weight[j], (((1,), (1,)), ((), ())), preferred_element_type=F32
         )
         scaled[j] = grad_normed * g
     for i in range(8):
@@ -176,15 +186,18 @@
     vmem = pl.BlockSpec(memory_space=pltpu.VMEM)
     return pl.pallas_call(
         _tokens_kernel,
-        in_specs=[pl.BlockSpec(memory_space=pltpu.SMEM)] + [vmem] * (5 + len(pieces)),
+        in_specs=[pl.BlockSpec(memory_space=pltpu.SMEM)]
+        + [vmem] * 5
+        + [pl.BlockSpec(memory_space=pltpu.HBM)] * len(pieces),
         out_specs=[vmem, pl.BlockSpec(memory_space=pltpu.HBM)],
         scratch_shapes=[
             pltpu.VMEM((rows, kvw), BF),
-            pltpu.VMEM((CHUNK, kvw), BF),
+            pltpu.VMEM((chunks, CHUNK, kvw), BF),
             pltpu.VMEM((rows, kvw), F32),
             pltpu.VMEM((chunks, rows, CHUNK), F32),
             pltpu.VMEM((chunks, rows, CHUNK), BF),
             pltpu.SemaphoreType.DMA((chunks,)),
+            pltpu.SemaphoreType.DMA((chunks, 8)),
         ],
         out_shape=[
             jax.ShapeDtypeStruct((rows, kvw), BF),

time: 179 us -> 180 us (level)
  no operation moved by 1% of the time
where the time goes in v1:
time: 180 us; the launch traced here: 179 us
  waiting for transfers between devices  69 us (38%)
  Pallas kernels  45.8 us (25%)
  starting transfers between devices  45.6 us (25%)
  local copies, waits for them, and re-layouts  11.8 us (7%)
  other arithmetic  6.03 us (3%)
    ppermute x28, waiting for transfers between devices, _send(): return lax.ppermute(v, AXES, _pairs(move))  46.5 us
    ppermute x28, starting transfers between devices, _send(): return lax.ppermute(v, AXES, _pairs(move))  31.2 us
    pallas_call x7, Pallas kernels, small_kernel(): pl.pallas_call(body, in_specs=[smem] * len(scalars) + [vmem] * len(arrays...  18 us
    pallas_call x1, Pallas kernels, token_work(): pl.pallas_call(_tokens_kernel, in_specs=[pl.BlockSpec(memory_space=pltpu....  16.8 us
    all_to_all x1, waiting for transfers between devices, local(): w_both = lax.all_to_all(to_shards, 'shard', 0, 0, tiled=True)  14.5 us
    pallas_call x1, Pallas kernels, weight_terms(): pl.pallas_call(lambda *refs: _terms_kernel(scale, *refs), in_specs=[pl.Bl...  11 us
    all_to_all x1, waiting for transfers between devices, local(): got = lax.all_to_all(to_owners, 'shard', 0, 0, tiled=True)  7.99 us
    all_to_all x1, starting transfers between devices, local(): w_both = lax.all_to_all(to_shards, 'shard', 0, 0, tiled=True)  7.2 us
  transfers between devices with their start and end apart: 30, of which 11 were waited for; matrix products, arithmetic and copies ran while one was open for 8% of the time, Pallas kernels for 24%

profile of v1, /device:TPU:2, one launch (start us, length us, event | category | flops | bytes accessed | tf_op | source)
XLA Modules:
  0.0 179.2 jit_solution(14090138767849984024)
XLA Ops:
  0.7 1.3 fusion.5
  2.5 1.1 pad_maximum_fusion
  3.6 7.2 %all-to-all-start = ((bf16[16,32,8,128]{3,2,1,0:T(8,128)(2,1)}), bf16[16,32,8,128]{3,2,1,0:T(8,128)(2,1)S(1)}, u32[]{:S(2)}, u32[]{:S(2)}) async-start(bf16[16,32,8,128]{3,2,1,0:T(8,128)(2,1)} %bitcast.19), calls=%async_computation | async-start | bytes 2097152 | tf_op jit(solution)/shard_map/all_to_all | solution.py:398
  10.8 0.5 collective-permute-start.13
  11.3 3.0 %multiply_reduce_fusion = f32[384]{0:T(512)S(1)} fusion(bf16[384,5120]{1,0:T(8,128)(2,1)} %refs_5_.1), kind=kLoop, calls=%fused_computation.3 | loop fusion | flops 5897856 | bytes 3933696 | tf_op jit(solution)/shard_map/reduce_sum | solution.py:53
  14.3 14.5 %all-to-all-done = bf16[16,32,8,128]{3,2,1,0:T(8,128)(2,1)S(1)} async-done(((bf16[16,32,8,128]{3,2,1,0:T(8,128)(2,1)}), bf16[16,32,8,128]{3,2,1,0:T(8,128)(2,1)S(1)}, u32[]{:S(2)}, u32[]{:S(2)}) %all-to-all-start) | async-done | bytes 1048608 | tf_op jit(solution)/shard_map/all_to_all | solution.py:398
  28.8 0.6 gather_fusion
  29.5 0.3 copy-done.7
  29.8 0.1 rsqrt.7.inv.refs_1_
  30.1 0.5 and_add_fusion
  30.6 0.9 collective-permute-done.12.refs_2_
  31.5 0.7 copy-done.13
  32.2 0.3 copy-done.9
  32.4 11.0 %weight_terms.1 = (bf16[5120,128]{1,0:T(8,128)(2,1)}, bf16[2560,128]{1,0:T(8,128)(2,1)}, bf16[2560,128]{1,0:T(8,128)(2,1)}, bf16[2560,128]{1,0:T(8,128)(2,1)}, b...) custom-call(s32[4]{0:T(128)} %get-tuple-element.47.refs_0_, f32[384,1]{1,0:T(8,128)} %copy-done.3, ...), custom_call_target="tpu_custom_call" | custom-call | tf_op jit(solution)/shard_map/weight_terms/pallas_call | solution.py:117
  43.4 1.6 collective-permute-start.16
  45.0 1.7 collective-permute-start.17
  46.6 1.8 %collective-permute-start.15 = (bf16[2560,128]{1,0:T(8,128)(2,1)}, bf16[2560,128]{1,0:T(8,128)(2,1)}, u32[]{:S(2)}, u32[]{:S(2)}) collective-permute-start(bf16[2560,128]{1,0:T(8,128)(2,1)} %get-tuple-element.26), channel_id=1, source_target_pairs={{0,3},{8,56},{16,19},{24,8},{32,35},{40,24},{48,51},{56,40},{1,0},... | collective-permute-start | bytes 1966088 | tf_op jit(solution)/shard_map/ppermute | solution.py:36
  48.4 1.7 collective-permute-start.1
  50.1 1.5 collective-permute-start.2
  51.7 0.5 add_and_fusion
  52.2 6.0 %collective-permute-done.1.three = bf16[40,32,128]{2,1,0:T(8,128)(2,1)S(1)} collective-permute-done((bf16[40,32,128]{2,1,0:T(8,128)(2,1)S(1)}, bf16[40,32,128]{2,1,0:T(8,128)(2,1)S(1)}, u32[]{:S(2)}, u32[]{:S(2)}) %collective-permute-start.1) | collective-permute-done | bytes 327712 | tf_op jit(solution)/shard_map/ppermute | solution.py:36
  58.2 6.0 %collective-permute-done.2.four = bf16[40,32,128]{2,1,0:T(8,128)(2,1)S(1)} collective-permute-done((bf16[40,32,128]{2,1,0:T(8,128)(2,1)S(1)}, bf16[40,32,128]{2,1,0:T(8,128)(2,1)S(1)}, u32[]{:S(2)}, u32[]{:S(2)}) %collective-permute-start.2) | collective-permute-done | bytes 327712 | tf_op jit(solution)/shard_map/ppermute | solution.py:36
  64.3 0.7 copy-done.12
  65.0 2.4 %shard_map.110 = bf16[40,4,32,128]{3,2,1,0:T(8,128)(2,1)} custom-call(s32[4]{0:T(128)} %get-tuple-element.51.index, bf16[40,32,128]{2,1,0:T(8,128)(2,1)} %copy-done.8, bf16[40,32,128]{2,1,0:T(8,128)(2,1)} %copy-done.10, bf16[40,32,128]{2,1,0:T(8,128)(2,1)} %copy-done.11, bf16[40,32,128]{2,1,0:T(8,128)(2,1)} %copy-done.12), custom_call_target="tpu_custom_call" | custom-call | tf_op jit(solution)/shard_map/pallas_call | solution.py:214
  67.4 1.6 collective-permute-start.3
  69.0 1.6 collective-permute-start.19
  70.6 2.9 %shard_map.111 = (bf16[2560,128]{1,0:T(8,128)(2,1)}, bf16[2560,128]{1,0:T(8,128)(2,1)}) custom-call(bf16[2560,128]{1,0:T(8,128)(2,1)} %get-tuple-element.27.one, bf16[2560,128]{1,0:T(8,128)(2,1)} %collective-permute-done.16.two, bf16[2560,128]{1,0:T(8,128)(2,1)} %get-tuple-element.29.three, bf16[2560,128]{1,0:T(8,128)(2,1)} %collective-permute-done.17.four), custom_call_target="tpu_custom_call" | custom-call | tf_op jit(solution)/shard_map/pallas_call | solution.py:214
  73.5 1.3 collective-permute-start.18
  74.8 2.0 %collective-permute-start.20 = (bf16[2560,128]{1,0:T(8,128)(2,1)}, bf16[2560,128]{1,0:T(8,128)(2,1)}, u32[]{:S(2)}, u32[]{:S(2)}) collective-permute-start(bf16[2560,128]{1,0:T(8,128)(2,1)} %get-tuple-element.33), channel_id=1, source_target_pairs={{0,3},{8,56},{16,19},{24,8},{32,35},{40,24},{48,51},{56,40},{1,0},... | collective-permute-start | bytes 1966088 | tf_op jit(solution)/shard_map/ppermute | solution.py:36
  76.8 0.4 collective-permute-start.4
  77.2 1.2 scatter_custom_fusion.block_of_slot
  78.4 0.1 convert_reduce_fusion
  78.5 15.0 %collective-permute-done.19 = bf16[2560,128]{1,0:T(8,128)(2,1)} collective-permute-done((bf16[2560,128]{1,0:T(8,128)(2,1)}, bf16[2560,128]{1,0:T(8,128)(2,1)}, u32[]{:S(2)}, u32[]{:S(2)}) %collective-permute-start.19) | collective-permute-done | bytes 655392 | tf_op jit(solution)/shard_map/ppermute | solution.py:36
  93.6 7.0 %collective-permute-done.18 = bf16[2560,128]{1,0:T(8,128)(2,1)} collective-permute-done((bf16[2560,128]{1,0:T(8,128)(2,1)}, bf16[2560,128]{1,0:T(8,128)(2,1)}, u32[]{:S(2)}, u32[]{:S(2)}) %collective-permute-start.18) | collective-permute-done | bytes 655392 | tf_op jit(solution)/shard_map/ppermute | solution.py:36
  100.6 3.5 %shard_map.112 = (bf16[40,32,128]{2,1,0:T(8,128)(2,1)}, bf16[40,32,128]{2,1,0:T(8,128)(2,1)}, bf16[40,32,128]{2,1,0:T(8,128)(2,1)}, bf16[40,32,128]{2,1,0:T(8,128)(2,1)}) custom-call(s32[4]{0:T(128)} %get-tuple-element.48.index, bf16[40,4,32,128]{3,2,1,0:T(8,128)(2,1)} %bitcast.60, bf16[20,4,32,128]{3,2,1,0:T(8,128)(2,1)} %bitcast.24.top_1, ...), custom_call_target="tpu_custom_call" | custom-call | tf_op jit(solution)/shard_map/pallas_call | solution.py:214
  104.1 1.5 collective-permute-start.21
  105.6 1.7 collective-permute-start.22
  107.4 0.3 collective-permute-start.23
  107.7 0.6 pad_maximum_fusion.1.bias
  108.3 2.6 %gather_fusion.1 = bf16[40,32,128]{2,1,0:T(8,128)(2,1)} fusion(bf16[128,32,128]{2,1,0:T(8,128)(2,1)} %bitcast.58, s32[1024]{0:T(1024)S(1)} %pad_clamp_fusion), kind=kCustom, calls=%fused_computation.1 | custom fusion | bytes 655520 | tf_op jit(solution)/shard_map/jit(_take)/gather | solution.py:402
  110.9 1.9 %collective-permute-done.21.two = bf16[40,32,128]{2,1,0:T(8,128)(2,1)} collective-permute-done((bf16[40,32,128]{2,1,0:T(8,128)(2,1)}, bf16[40,32,128]{2,1,0:T(8,128)(2,1)}, u32[]{:S(2)}, u32[]{:S(2)}) %collective-permute-start.21) | collective-permute-done | bytes 327712 | tf_op jit(solution)/shard_map/ppermute | solution.py:36
  112.7 0.3 collective-permute-done.22.three
  113.0 3.2 %collective-permute-done.23.four = bf16[40,32,128]{2,1,0:T(8,128)(2,1)} collective-permute-done((bf16[40,32,128]{2,1,0:T(8,128)(2,1)}, bf16[40,32,128]{2,1,0:T(8,128)(2,1)}, u32[]{:S(2)}, u32[]{:S(2)}) %collective-permute-start.23) | collective-permute-done | bytes 327712 | tf_op jit(solution)/shard_map/ppermute | solution.py:36
  116.3 2.6 %shard_map.113 = bf16[16,184,128]{2,1,0:T(8,128)(2,1)} custom-call(s32[64]{0:T(128)} %scatter_custom_fusion.block_of_slot, s32[1]{0:T(128)} %bitcast.22.row_block, bf16[40,32,128]{2,1,0:T(8,128)(2,1)} %get-tuple-element.34.one, bf16[40,32,128]{2,1,0:T(8,128)(2,1)} %collective-permute-done.21.two, bf16[40,32,128]{2,1,0:T(8,128)(2,1)} %collective-permute-done.22.three, ...), custom_call_target="tpu_custom_call" | custom-call | tf_op jit(solution)/shard_map/pallas_call | solution.py:214
  118.9 7.2 %all-to-all-start.1 = ((bf16[16,184,128]{2,1,0:T(8,128)(2,1)}), bf16[16,184,128]{2,1,0:T(8,128)(2,1)}, u32[]{:S(2)}, u32[]{:S(2)}) async-start(bf16[16,184,128]{2,1,0:T(8,128)(2,1)} %shard_map.113), calls=%async_computation.1 | async-start | bytes 1507328 | tf_op jit(solution)/shard_map/all_to_all | solution.py:430
  126.0 0.9 slice.22
  126.9 0.4 collective-permute-start.5
  127.3 1.3 collective-permute-start.7
  128.6 2.0 %slice.23 = bf16[2560,128]{1,0:T(8,128)(2,1)} slice(bf16[5120,128]{1,0:T(8,128)(2,1)} %collective-permute-done.4.rest_2_), slice={[2560:5120], [0:128]} | slice | bytes 1310720 | tf_op jit(solution)/shard_map/slice | solution.py:409
  130.6 1.8 %collective-permute-start.6 = (bf16[2560,128]{1,0:T(8,128)(2,1)}, bf16[2560,128]{1,0:T(8,128)(2,1)}, u32[]{:S(2)}, u32[]{:S(2)}) collective-permute-start(bf16[2560,128]{1,0:T(8,128)(2,1)} %slice.23), channel_id=1, source_target_pairs={{0,3},{8,56},{16,19},{24,8},{32,35},{40,24},{48,51},{56,40},{1,0},... | collective-permute-start | bytes 1966088 | tf_op jit(solution)/shard_map/ppermute | solution.py:36
  132.4 0.2 collective-permute-start.8
  132.6 0.3 collective-permute-start.9
  132.9 8.0 %all-to-all-done.1.r_0_ = bf16[16,184,128]{2,1,0:T(8,128)(2,1)} async-done(((bf16[16,184,128]{2,1,0:T(8,128)(2,1)}), bf16[16,184,128]{2,1,0:T(8,128)(2,1)}, u32[]{:S(2)}, u32[]{:S(2)}) %all-to-all-start.1) | async-done | bytes 753696 | tf_op jit(solution)/shard_map/all_to_all | solution.py:430
  140.9 1.9 %shard_map.114.r_0_ = bf16[1120,128]{1,0:T(8,128)(2,1)} custom-call(bf16[16,184,128]{2,1,0:T(8,128)(2,1)} %all-to-all-done.1.r_0_), custom_call_target="tpu_custom_call" | custom-call | tf_op jit(solution)/shard_map/pallas_call | solution.py:214
  142.9 2.5 %collective-permute-start.10 = (bf16[2560,128]{1,0:T(8,128)(2,1)}, bf16[2560,128]{1,0:T(8,128)(2,1)}, u32[]{:S(2)}, u32[]{:S(2)}) collective-permute-start(bf16[2560,128]{1,0:T(8,128)(2,1)} %collective-permute-done.5.rest_3_), channel_id=1, source_target_pairs={{0,8},{8,0},{16,24},{24,16},{32,40},{40,32},{48,56},{56,48},{1,9},... | collective-permute-start | bytes 1966088 | tf_op jit(solution)/shard_map/ppermute | solution.py:36
  145.3 6.1 %collective-permute-done.24.r_1_ = bf16[1120,128]{1,0:T(8,128)(2,1)} collective-permute-done((bf16[1120,128]{1,0:T(8,128)(2,1)}, bf16[1120,128]{1,0:T(8,128)(2,1)}, u32[]{:S(2)}, u32[]{:S(2)}) %collective-permute-start.24) | collective-permute-done | bytes 286752 | tf_op jit(solution)/shard_map/ppermute | solution.py:36
  151.4 1.3 collective-permute-start.11
  152.7 1.8 %shard_map.115.r_1_ = bf16[1120,128]{1,0:T(8,128)(2,1)} custom-call(bf16[1120,128]{1,0:T(8,128)(2,1)} %shard_map.114.r_0_, bf16[1120,128]{1,0:T(8,128)(2,1)} %collective-permute-done.24.r_1_), custom_call_target="tpu_custom_call" | custom-call | tf_op jit(solution)/shard_map/pallas_call | solution.py:214
  154.5 0.4 collective-permute-start.25
  154.9 2.9 %collective-permute-start.26 = (bf16[1120,128]{1,0:T(8,128)(2,1)}, bf16[1120,128]{1,0:T(8,128)(2,1)}, u32[]{:S(2)}, u32[]{:S(2)}) collective-permute-start(bf16[1120,128]{1,0:T(8,128)(2,1)} %shard_map.115.r_1_), channel_id=1, source_target_pairs={{0,3},{8,11},{16,19},{24,27},{32,35},{40,43},{48,51},{56,59},{1,0}... | collective-permute-start | bytes 860168 | tf_op jit(solution)/shard_map/ppermute | solution.py:36
  157.8 0.8 collective-permute-start.27
  158.7 0.9 copy-done.4
  159.6 16.8 %token_work.1 = (bf16[384,1024]{1,0:T(8,128)(2,1)}, bf16[384,5120]{1,0:T(8,128)(2,1)}) custom-call(s32[8]{0:T(128)S(1)} %pad_add_fusion.tiles, bf16[384,5120]{1,0:T(8,128)(2,1)} %refs_5_.1, f32[384,1]{1,0:T(8,128)S(1)} %copy-done.4, f32[1,5120]{1,0:T(1,128)S(1)} %bitcast.55, f32[1,1024]{1,0:T(1,128)S(1)} %bitcast.56, bf16[384,1024]{1,0:T(8,128)(2,1)S(1)} %copy-done.1, ...), custom_call_target="tpu_custom_call" | custom-call | tf_op jit(solution)/shard_map/token_work/pallas_call | solution.py:187
  176.5 2.8 %shard_map.116 = (f32[512,1024]{1,0:T(8,128)}, f32[40,128]{1,0:T(8,128)}, f32[8,128]{1,0:T(8,128)}) custom-call(s32[4]{0:T(128)} %get-tuple-element.50.r_0_, bf16[1120,128]{1,0:T(8,128)(2,1)} %shard_map.115.r_1_, bf16[1120,128]{1,0:T(8,128)(2,1)} %collective-permute-done.25.r_2_, bf16[1120,128]{1,0:T(8,128)(2,1)} %collective-permute-done.26.r_3_, ...), custom_call_target="tpu_custom_call" | custom-call | tf_op jit(solution)/shard_map/pallas_call | solution.py:214
  (69 shorter events, 0.8 us)
Async XLA Ops:
  0.6 30.9 %collective-permute-start.14 = (bf16[384,5120]{1,0:T(8,128)(2,1)}, bf16[384,5120]{1,0:T(8,128)(2,1)}, u32[]{:S(2)}, u32[]{:S(2)}) collective-permute-start(bf16[384,5120]{1,0:T(8,128)(2,1)} %refs_5_.1), channel_id=1, source_target_pairs={{0,8},{8,0},{16,24},{24,16},{32,40},{40,32},{48,56},{56,48},{1,9},... | collective-permute-start | bytes 11796488 | tf_op jit(solution)/shard_map/ppermute | solution.py:36
  3.6 7.2 %copy-start = (bf16[384,1024]{1,0:T(8,128)(2,1)S(1)}, bf16[384,1024]{1,0:T(8,128)(2,1)}, u32[]{:S(2)}) copy-start(bf16[384,1024]{1,0:T(8,128)(2,1)} %refs_3_.1) | copy-start | bytes 2359300
  3.6 7.7 %copy-start.14 = (s32[40]{0:T(128)S(1)}, s32[40]{0:T(128)}, u32[]{:S(2)}) copy-start(s32[40]{0:T(128)} %param.12) | copy-start | bytes 484
  3.6 25.2 %all-to-all-start = ((bf16[16,32,8,128]{3,2,1,0:T(8,128)(2,1)}), bf16[16,32,8,128]{3,2,1,0:T(8,128)(2,1)S(1)}, u32[]{:S(2)}, u32[]{:S(2)}) async-start(bf16[16,32,8,128]{3,2,1,0:T(8,128)(2,1)} %bitcast.19), calls=%async_computation | async-start | bytes 2097152 | tf_op jit(solution)/shard_map/all_to_all | solution.py:398
  10.8 20.7 %collective-permute-start.13 = (bf16[384,1024]{1,0:T(8,128)(2,1)S(1)}, bf16[384,1024]{1,0:T(8,128)(2,1)S(1)}, u32[]{:S(2)}, u32[]{:S(2)}) collective-permute-start(bf16[384,1024]{1,0:T(8,128)(2,1)S(1)} %copy-done), channel_id=1, source_target_pairs={{0,8},{8,0},{16,24},{24,16},{32,40},{40,32},{48,56},{56,48},{1,9},... | collective-permute-start | bytes 2359304 | tf_op jit(solution)/shard_map/ppermute | solution.py:36
  11.3 18.8 %copy-start.15 = (s32[4]{0:T(128)S(1)}, s32[4]{0:T(128)}, u32[]{:S(2)}) copy-start(s32[4]{0:T(128)} %constant.59.clone) | copy-start | bytes 52
  28.8 1.0 copy-start.7
  29.4 20.7 %copy-start.8 = (bf16[40,32,128]{2,1,0:T(8,128)(2,1)}, bf16[40,32,128]{2,1,0:T(8,128)(2,1)S(1)}, u32[]{:S(2)}) copy-start(bf16[40,32,128]{2,1,0:T(8,128)(2,1)S(1)} %gather_fusion) | copy-start | bytes 983044
  29.4 20.7 %collective-permute-start = (bf16[40,32,128]{2,1,0:T(8,128)(2,1)S(1)}, bf16[40,32,128]{2,1,0:T(8,128)(2,1)S(1)}, u32[]{:S(2)}, u32[]{:S(2)}) collective-permute-start(bf16[40,32,128]{2,1,0:T(8,128)(2,1)S(1)} %gather_fusion), channel_id=1, source_target_pairs={{0,4},{8,12},{16,20},{24,28},{32,36},{40,44},{48,52},{56,60},{1,5}... | collective-permute-start | bytes 983048 | tf_op jit(solution)/shard_map/ppermute | solution.py:36
  30.0 1.5 copy-start.3
  30.0 1.5 collective-permute-start.12
  31.5 0.7 copy-start.13
  31.5 0.9 copy-start.9
  32.4 19.2 %copy-start.16 = (s32[4]{0:T(128)S(1)}, s32[4]{0:T(128)}, u32[]{:S(2)}) copy-start(s32[4]{0:T(128)} %constant.60) | copy-start | bytes 52
  43.4 27.2 %collective-permute-start.16 = (bf16[2560,128]{1,0:T(8,128)(2,1)}, bf16[2560,128]{1,0:T(8,128)(2,1)}, u32[]{:S(2)}, u32[]{:S(2)}) collective-permute-start(bf16[2560,128]{1,0:T(8,128)(2,1)} %get-tuple-element.28), channel_id=1, source_target_pairs={{0,1},{8,24},{16,17},{24,40},{32,33},{40,56},{48,49},{56,8},{1,2},... | collective-permute-start | bytes 1966088 | tf_op jit(solution)/shard_map/ppermute | solution.py:36
  45.0 25.6 %collective-permute-start.17 = (bf16[2560,128]{1,0:T(8,128)(2,1)}, bf16[2560,128]{1,0:T(8,128)(2,1)}, u32[]{:S(2)}, u32[]{:S(2)}) collective-permute-start(bf16[2560,128]{1,0:T(8,128)(2,1)} %get-tuple-element.30), channel_id=1, source_target_pairs={{0,3},{8,56},{16,19},{24,8},{32,35},{40,24},{48,51},{56,40},{1,0},... | collective-permute-start | bytes 1966088 | tf_op jit(solution)/shard_map/ppermute | solution.py:36
  46.6 30.1 %collective-permute-start.15 = (bf16[2560,128]{1,0:T(8,128)(2,1)}, bf16[2560,128]{1,0:T(8,128)(2,1)}, u32[]{:S(2)}, u32[]{:S(2)}) collective-permute-start(bf16[2560,128]{1,0:T(8,128)(2,1)} %get-tuple-element.26), channel_id=1, source_target_pairs={{0,3},{8,56},{16,19},{24,8},{32,35},{40,24},{48,51},{56,40},{1,0},... | collective-permute-start | bytes 1966088 | tf_op jit(solution)/shard_map/ppermute | solution.py:36
  48.4 9.8 %collective-permute-start.1 = (bf16[40,32,128]{2,1,0:T(8,128)(2,1)S(1)}, bf16[40,32,128]{2,1,0:T(8,128)(2,1)S(1)}, u32[]{:S(2)}, u32[]{:S(2)}) collective-permute-start(bf16[40,32,128]{2,1,0:T(8,128)(2,1)S(1)} %gather_fusion), channel_id=1, source_target_pairs={{0,68},{8,76},{16,84},{24,92},{32,100},{40,108},{48,116},{56,124},... | collective-permute-start | bytes 983048 | tf_op jit(solution)/shard_map/ppermute | solution.py:36
  50.1 14.1 %copy-start.10 = (bf16[40,32,128]{2,1,0:T(8,128)(2,1)}, bf16[40,32,128]{2,1,0:T(8,128)(2,1)S(1)}, u32[]{:S(2)}) copy-start(bf16[40,32,128]{2,1,0:T(8,128)(2,1)S(1)} %collective-permute-done.two) | copy-start | bytes 983044
  50.1 14.1 %collective-permute-start.2 = (bf16[40,32,128]{2,1,0:T(8,128)(2,1)S(1)}, bf16[40,32,128]{2,1,0:T(8,128)(2,1)S(1)}, u32[]{:S(2)}, u32[]{:S(2)}) collective-permute-start(bf16[40,32,128]{2,1,0:T(8,128)(2,1)S(1)} %gather_fusion), channel_id=1, source_target_pairs={{0,64},{8,72},{16,80},{24,88},{32,96},{40,104},{48,112},{56,120},{... | collective-permute-start | bytes 983048 | tf_op jit(solution)/shard_map/ppermute | solution.py:36
  58.2 6.0 %copy-start.11 = (bf16[40,32,128]{2,1,0:T(8,128)(2,1)}, bf16[40,32,128]{2,1,0:T(8,128)(2,1)S(1)}, u32[]{:S(2)}) copy-start(bf16[40,32,128]{2,1,0:T(8,128)(2,1)S(1)} %collective-permute-done.1.three) | copy-start | bytes 983044
  64.3 0.7 copy-start.12
  67.4 9.3 %copy-start.2 = (bf16[40,4,32,128]{3,2,1,0:T(8,128)(2,1)S(1)}, bf16[40,4,32,128]{3,2,1,0:T(8,128)(2,1)}, u32[]{:S(2)}) copy-start(bf16[40,4,32,128]{3,2,1,0:T(8,128)(2,1)} %shard_map.110) | copy-start | bytes 3932164
  67.4 11.0 %copy-start.1 = (bf16[384,1024]{1,0:T(8,128)(2,1)S(1)}, bf16[384,1024]{1,0:T(8,128)(2,1)}, u32[]{:S(2)}) copy-start(bf16[384,1024]{1,0:T(8,128)(2,1)} %refs_3_.1) | copy-start | bytes 2359300
  67.4 58.6 %collective-permute-start.3 = (bf16[5120,128]{1,0:T(8,128)(2,1)}, bf16[5120,128]{1,0:T(8,128)(2,1)S(1)}, u32[]{:S(2)}, u32[]{:S(2)}) collective-permute-start(bf16[5120,128]{1,0:T(8,128)(2,1)} %bitcast.49), channel_id=1, source_target_pairs={{0,1},{8,24},{16,17},{24,40},{32,33},{40,56},{48,49},{56,8},{1,2},... | collective-permute-start | bytes 3932168 | tf_op jit(solution)/shard_map/ppermute | solution.py:36
  69.0 24.6 %collective-permute-start.19 = (bf16[2560,128]{1,0:T(8,128)(2,1)}, bf16[2560,128]{1,0:T(8,128)(2,1)}, u32[]{:S(2)}, u32[]{:S(2)}) collective-permute-start(bf16[2560,128]{1,0:T(8,128)(2,1)} %get-tuple-element.32), channel_id=1, source_target_pairs={{0,1},{8,24},{16,17},{24,40},{32,33},{40,56},{48,49},{56,8},{1,2},... | collective-permute-start | bytes 1966088 | tf_op jit(solution)/shard_map/ppermute | solution.py:36
  73.5 27.1 %collective-permute-start.18 = (bf16[2560,128]{1,0:T(8,128)(2,1)}, bf16[2560,128]{1,0:T(8,128)(2,1)}, u32[]{:S(2)}, u32[]{:S(2)}) collective-permute-start(bf16[2560,128]{1,0:T(8,128)(2,1)} %get-tuple-element.31), channel_id=1, source_target_pairs={{0,1},{8,24},{16,17},{24,40},{32,33},{40,56},{48,49},{56,8},{1,2},... | collective-permute-start | bytes 1966088 | tf_op jit(solution)/shard_map/ppermute | solution.py:36
  74.8 25.8 %collective-permute-start.20 = (bf16[2560,128]{1,0:T(8,128)(2,1)}, bf16[2560,128]{1,0:T(8,128)(2,1)}, u32[]{:S(2)}, u32[]{:S(2)}) collective-permute-start(bf16[2560,128]{1,0:T(8,128)(2,1)} %get-tuple-element.33), channel_id=1, source_target_pairs={{0,3},{8,56},{16,19},{24,8},{32,35},{40,24},{48,51},{56,40},{1,0},... | collective-permute-start | bytes 1966088 | tf_op jit(solution)/shard_map/ppermute | solution.py:36
  76.8 51.9 %collective-permute-start.4 = (bf16[5120,128]{1,0:T(8,128)(2,1)S(1)}, bf16[5120,128]{1,0:T(8,128)(2,1)}, u32[]{:S(2)}, u32[]{:S(2)}) collective-permute-start(bf16[5120,128]{1,0:T(8,128)(2,1)S(1)} %bitcast.50), channel_id=1, source_target_pairs={{0,3},{8,56},{16,19},{24,8},{32,35},{40,24},{48,51},{56,40},{1,0},... | collective-permute-start | bytes 3932168 | tf_op jit(solution)/shard_map/ppermute | solution.py:36
  104.1 8.6 %collective-permute-start.21 = (bf16[40,32,128]{2,1,0:T(8,128)(2,1)}, bf16[40,32,128]{2,1,0:T(8,128)(2,1)}, u32[]{:S(2)}, u32[]{:S(2)}) collective-permute-start(bf16[40,32,128]{2,1,0:T(8,128)(2,1)} %get-tuple-element.35), channel_id=1, source_target_pairs={{0,16},{8,9},{16,32},{24,25},{32,48},{40,41},{48,0},{56,57},{1,17}... | collective-permute-start | bytes 983048 | tf_op jit(solution)/shard_map/ppermute | solution.py:36
  105.6 7.4 %collective-permute-start.22 = (bf16[40,32,128]{2,1,0:T(8,128)(2,1)}, bf16[40,32,128]{2,1,0:T(8,128)(2,1)}, u32[]{:S(2)}, u32[]{:S(2)}) collective-permute-start(bf16[40,32,128]{2,1,0:T(8,128)(2,1)} %get-tuple-element.36), channel_id=1, source_target_pairs={{0,48},{8,11},{16,0},{24,27},{32,16},{40,43},{48,32},{56,59},{1,49... | collective-permute-start | bytes 983048 | tf_op jit(solution)/shard_map/ppermute | solution.py:36
  107.4 8.9 %collective-permute-start.23 = (bf16[40,32,128]{2,1,0:T(8,128)(2,1)}, bf16[40,32,128]{2,1,0:T(8,128)(2,1)}, u32[]{:S(2)}, u32[]{:S(2)}) collective-permute-start(bf16[40,32,128]{2,1,0:T(8,128)(2,1)} %get-tuple-element.37), channel_id=1, source_target_pairs={{0,32},{8,10},{16,48},{24,26},{32,0},{40,42},{48,16},{56,58},{1,33... | collective-permute-start | bytes 983048 | tf_op jit(solution)/shard_map/ppermute | solution.py:36
  118.9 22.1 %all-to-all-start.1 = ((bf16[16,184,128]{2,1,0:T(8,128)(2,1)}), bf16[16,184,128]{2,1,0:T(8,128)(2,1)}, u32[]{:S(2)}, u32[]{:S(2)}) async-start(bf16[16,184,128]{2,1,0:T(8,128)(2,1)} %shard_map.113), calls=%async_computation.1 | async-start | bytes 1507328 | tf_op jit(solution)/shard_map/all_to_all | solution.py:430
  126.9 31.7 %copy-start.5 = (f32[5120]{0:T(1024)S(1)}, f32[5120]{0:T(1024)}, u32[]{:S(2)}) copy-start(f32[5120]{0:T(1024)} %param.8) | copy-start | bytes 61444
  126.9 31.7 %copy-start.6 = (f32[1024]{0:T(1024)S(1)}, f32[1024]{0:T(1024)}, u32[]{:S(2)}) copy-start(f32[1024]{0:T(1024)} %param.9) | copy-start | bytes 12292
  126.9 15.9 %collective-permute-start.5 = (bf16[2560,128]{1,0:T(8,128)(2,1)}, bf16[2560,128]{1,0:T(8,128)(2,1)}, u32[]{:S(2)}, u32[]{:S(2)}) collective-permute-start(bf16[2560,128]{1,0:T(8,128)(2,1)} %slice.22), channel_id=1, source_target_pairs={{0,1},{8,24},{16,17},{24,40},{32,33},{40,56},{48,49},{56,8},{1,2},... | collective-permute-start | bytes 1966088 | tf_op jit(solution)/shard_map/ppermute | solution.py:36
  127.3 27.3 %collective-permute-start.7 = (bf16[5120,128]{1,0:T(8,128)(2,1)S(1)}, bf16[5120,128]{1,0:T(8,128)(2,1)}, u32[]{:S(2)}, u32[]{:S(2)}) collective-permute-start(bf16[5120,128]{1,0:T(8,128)(2,1)S(1)} %bitcast.51), channel_id=1, source_target_pairs={{0,8},{8,0},{16,24},{24,16},{32,40},{40,32},{48,56},{56,48},{1,9},... | collective-permute-start | bytes 3932168 | tf_op jit(solution)/shard_map/ppermute | solution.py:36
  130.6 12.3 %collective-permute-start.6 = (bf16[2560,128]{1,0:T(8,128)(2,1)}, bf16[2560,128]{1,0:T(8,128)(2,1)}, u32[]{:S(2)}, u32[]{:S(2)}) collective-permute-start(bf16[2560,128]{1,0:T(8,128)(2,1)} %slice.23), channel_id=1, source_target_pairs={{0,3},{8,56},{16,19},{24,8},{32,35},{40,24},{48,51},{56,40},{1,0},... | collective-permute-start | bytes 1966088 | tf_op jit(solution)/shard_map/ppermute | solution.py:36
  132.4 26.2 %collective-permute-start.8 = (bf16[5120,128]{1,0:T(8,128)(2,1)S(1)}, bf16[5120,128]{1,0:T(8,128)(2,1)}, u32[]{:S(2)}, u32[]{:S(2)}) collective-permute-start(bf16[5120,128]{1,0:T(8,128)(2,1)S(1)} %collective-permute-done.3.rest_1_), channel_id=1, source_target_pairs={{0,8},{8,0},{16,24},{24,16},{32,40},{40,32},{48,56},{56,48},{1,9},... | collective-permute-start | bytes 3932168 | tf_op jit(solution)/shard_map/ppermute | solution.py:36
  132.6 26.1 %collective-permute-start.9 = (bf16[5120,128]{1,0:T(8,128)(2,1)}, bf16[5120,128]{1,0:T(8,128)(2,1)}, u32[]{:S(2)}, u32[]{:S(2)}) collective-permute-start(bf16[5120,128]{1,0:T(8,128)(2,1)} %collective-permute-done.4.rest_2_), channel_id=1, source_target_pairs={{0,8},{8,0},{16,24},{24,16},{32,40},{40,32},{48,56},{56,48},{1,9},... | collective-permute-start | bytes 3932168 | tf_op jit(solution)/shard_map/ppermute | solution.py:36
  142.8 8.5 %collective-permute-start.24 = (bf16[1120,128]{1,0:T(8,128)(2,1)}, bf16[1120,128]{1,0:T(8,128)(2,1)}, u32[]{:S(2)}, u32[]{:S(2)}) collective-permute-start(bf16[1120,128]{1,0:T(8,128)(2,1)} %shard_map.114.r_0_), channel_id=1, source_target_pairs={{0,4},{8,12},{16,20},{24,28},{32,36},{40,44},{48,52},{56,60},{1,5}... | collective-permute-start | bytes 860168 | tf_op jit(solution)/shard_map/ppermute | solution.py:36
  142.9 12.1 %collective-permute-start.10 = (bf16[2560,128]{1,0:T(8,128)(2,1)}, bf16[2560,128]{1,0:T(8,128)(2,1)}, u32[]{:S(2)}, u32[]{:S(2)}) collective-permute-start(bf16[2560,128]{1,0:T(8,128)(2,1)} %collective-permute-done.5.rest_3_), channel_id=1, source_target_pairs={{0,8},{8,0},{16,24},{24,16},{32,40},{40,32},{48,56},{56,48},{1,9},... | collective-permute-start | bytes 1966088 | tf_op jit(solution)/shard_map/ppermute | solution.py:36
  151.4 6.4 %collective-permute-start.11 = (bf16[2560,128]{1,0:T(8,128)(2,1)}, bf16[2560,128]{1,0:T(8,128)(2,1)}, u32[]{:S(2)}, u32[]{:S(2)}) collective-permute-start(bf16[2560,128]{1,0:T(8,128)(2,1)} %collective-permute-done.6.rest_4_), channel_id=1, source_target_pairs={{0,8},{8,0},{16,24},{24,16},{32,40},{40,32},{48,56},{56,48},{1,9},... | collective-permute-start | bytes 1966088 | tf_op jit(solution)/shard_map/ppermute | solution.py:36
  154.5 21.9 %collective-permute-start.25 = (bf16[1120,128]{1,0:T(8,128)(2,1)}, bf16[1120,128]{1,0:T(8,128)(2,1)}, u32[]{:S(2)}, u32[]{:S(2)}) collective-permute-start(bf16[1120,128]{1,0:T(8,128)(2,1)} %shard_map.115.r_1_), channel_id=1, source_target_pairs={{0,1},{8,9},{16,17},{24,25},{32,33},{40,41},{48,49},{56,57},{1,2},... | collective-permute-start | bytes 860168 | tf_op jit(solution)/shard_map/ppermute | solution.py:36
  154.9 21.5 %collective-permute-start.26 = (bf16[1120,128]{1,0:T(8,128)(2,1)}, bf16[1120,128]{1,0:T(8,128)(2,1)}, u32[]{:S(2)}, u32[]{:S(2)}) collective-permute-start(bf16[1120,128]{1,0:T(8,128)(2,1)} %shard_map.115.r_1_), channel_id=1, source_target_pairs={{0,3},{8,11},{16,19},{24,27},{32,35},{40,43},{48,51},{56,59},{1,0}... | collective-permute-start | bytes 860168 | tf_op jit(solution)/shard_map/ppermute | solution.py:36
  157.8 18.7 %collective-permute-start.27 = (bf16[1120,128]{1,0:T(8,128)(2,1)}, bf16[1120,128]{1,0:T(8,128)(2,1)}, u32[]{:S(2)}, u32[]{:S(2)}) collective-permute-start(bf16[1120,128]{1,0:T(8,128)(2,1)} %shard_map.115.r_1_), channel_id=1, source_target_pairs={{0,2},{8,10},{16,18},{24,26},{32,34},{40,42},{48,50},{56,58},{1,3}... | collective-permute-start | bytes 860168 | tf_op jit(solution)/shard_map/ppermute | solution.py:36
  158.7 0.9 copy-start.4
